TPU v7x, 32 devices: a whole 2x2x4 slice. The times are simulated.
32 devices in a mesh: dp: 8 (over z, y), ctx: 4 (over x, core).
Axes of the slice: x: 2, y: 2, z: 4, core: 2. Of those that a mesh axis runs over, the one named last changes fastest.
Arguments:
- tokens: bfloat16 [16, 1024, 1024], P('dp', 'ctx'), may hold values from -6 to 6
- first_values: bfloat16 [16, 1024, 1024], P('dp', 'ctx'), may hold values from -6 to 6
- cotangent: bfloat16 [16, 1024, 1024], P('dp', 'ctx'), may hold values from -6 to 6
- segment_ids: int32 [16, 1024], P('dp'), may hold values from 0 to 4, as said below
- attn_gain: bfloat16 [1024], P(('dp', 'ctx')), may hold values from 0.5 to 1.5
- w_query: bfloat16 [1024, 1024], P(('dp', 'ctx')), may hold values from -0.1875 to 0.1875
- w_key: bfloat16 [1024, 1024], P(('dp', 'ctx')), may hold values from -0.1875 to 0.1875
- w_value: bfloat16 [1024, 1024], P(('dp', 'ctx')), may hold values from -0.1875 to 0.1875
- w_out: bfloat16 [1024, 1024], P(('dp', 'ctx')), may hold values from -1 to 1
- ffn_gain: bfloat16 [1024], P(('dp', 'ctx')), may hold values from 0.5 to 1.5
- gate_weight: bfloat16 [1024, 2816], P(('dp', 'ctx')), may hold values from -0.1875 to 0.1875
- up_weight: bfloat16 [1024, 2816], P(('dp', 'ctx')), may hold values from -0.1875 to 0.1875
- down_weight: bfloat16 [2816, 1024], P(('dp', 'ctx')), may hold values from -0.21875 to 0.21875
Outputs:
- output: bfloat16 [16, 1024, 1024], P('dp', 'ctx')
- tokens_grad: float32 [16, 1024, 1024], P('dp', 'ctx')
- first_values_grad: float32 [16, 1024, 1024], P('dp', 'ctx')
- attn_gain_grad: float32 [1024], P(('dp', 'ctx'))
- query_grad: float32 [1024, 1024], P(('dp', 'ctx'))
- key_grad: float32 [1024, 1024], P(('dp', 'ctx'))
- value_grad: float32 [1024, 1024], P(('dp', 'ctx'))
- out_grad: float32 [1024, 1024], P(('dp', 'ctx'))
- ffn_gain_grad: float32 [1024], P(('dp', 'ctx'))
- gate_grad: float32 [1024, 2816], P(('dp', 'ctx'))
- up_grad: float32 [1024, 2816], P(('dp', 'ctx'))
- down_grad: float32 [2816, 1024], P(('dp', 'ctx'))
Inputs may be any that keep to these rules, and one draw needn't show every extreme that they name: `segment_ids`: along each sequence the ids start at 0 and rise by one where a document begins; every document but a sequence's last holds 60 to 800 tokens, and each sequence holds at least one document of exactly 800 tokens.
All inputs are finite; a program needn't handle non-finite values.
Results may differ from a plain program's by a relative error of at most 0.017.
Values may be sent and summed in bfloat16 or wider, within the bound.
A program may use at most 192 MiB of HBM per device.

v0:
```python
import functools
import jax
import jax.numpy as jnp
from jax import lax
from jax.experimental import pallas as pl
from jax.experimental.pallas import tpu as pltpu
from jax.sharding import PartitionSpec as P

HEADS = 16
HEAD_DIM = 64
MESH_ID = pl.DeviceIdType.MESH

epsilon = 1e-05
rope_base = 10000.0
score_scale = 0.125
masked_score = -1e30


def inverse_rms(values):
    return lax.rsqrt(jnp.mean(values * values, axis=-1, keepdims=True) + epsilon)


def swish(values):
    return values * jax.nn.sigmoid(values)


def first_half(shape):
    return lax.broadcasted_iota(jnp.int32, shape, len(shape) - 1) % HEAD_DIM < HEAD_DIM // 2


def swap_halves(values):
    return jnp.where(
        first_half(values.shape), pltpu.roll(values, 96, 1), pltpu.roll(values, 32, 1)
    )


def turned(values, cos_table, sin_table, sign):
    return values * cos_table + sign * (swap_halves(values) * sin_table)


def tables(segment_ids, rank, rows):
    seqs, length = segment_ids.shape
    places = jnp.arange(length, dtype=jnp.int32)
    edges = jnp.concatenate(
        [jnp.ones((seqs, 1), dtype=jnp.bool_), segment_ids[:, 1:] != segment_ids[:, :-1]], axis=1
    )
    starts = lax.cummax(jnp.where(edges, places[None, :], 0), axis=1)
    starts = lax.dynamic_slice_in_dim(starts, rank * rows, rows, 1)
    local = rank * rows + jnp.arange(rows, dtype=jnp.int32) - starts
    lane = jnp.arange(128, dtype=jnp.int32)
    half = HEAD_DIM // 2
    frequency = rope_base ** (-(lane % half).astype(jnp.float32) * 2.0 / HEAD_DIM)
    angles = local.astype(jnp.float32).reshape(seqs * rows, 1) * frequency
    sign = jnp.where(lane % HEAD_DIM < half, -1.0, 1.0)
    return starts.reshape(seqs, 1, rows), jnp.cos(angles), jnp.sin(angles) * sign


def normalise(tok, gain, normed):
    rows = tok.shape[0]

    @pl.loop(0, rows // 64)
    def _(i):
        at = pl.ds(pl.multiple_of(i * 64, 64), 64)
        values = tok[at, :].astype(jnp.float32)
        normed[at, :] = (values * inverse_rms(values) * gain).astype(jnp.bfloat16)


def columns_of(weight, lanes):
    block = weight[:, :, lanes]
    if block.shape[1] % 16:
        block = block.astype(jnp.float32)
    return block.reshape(block.shape[0] * block.shape[1], block.shape[2]).astype(jnp.bfloat16)


def project(normed, first, wq, wk, wv, cos_ref, sin_ref, query, pair):
    f32, bf16 = jnp.float32, jnp.bfloat16
    seqs, rows, width = query.shape

    @pl.loop(0, width // 256)
    def _(i):
        lanes = pl.ds(pl.multiple_of(i * 256, 256), 256)
        n1 = normed[...]
        cos_table, sin_table = cos_ref[...], sin_ref[...]
        queries = jnp.dot(n1, columns_of(wq, lanes), preferred_element_type=f32)
        keys = jnp.dot(n1, columns_of(wk, lanes), preferred_element_type=f32)
        values = jnp.dot(n1, columns_of(wv, lanes), preferred_element_type=f32)
        mixed = (0.5 * values + 0.5 * first[:, lanes].astype(f32)).astype(bf16)
        for half in range(2):
            part = slice(half * 128, half * 128 + 128)
            at = pl.ds(pl.multiple_of(i * 256 + half * 128, 128), 128)
            q = turned(queries[:, part], cos_table, sin_table, 1.0).astype(bf16)
            k = turned(keys[:, part], cos_table, sin_table, 1.0).astype(bf16)
            for s in range(seqs):
                query[s, :, at] = q[s * rows : (s + 1) * rows]
                pair[0, s, :, at] = k[s * rows : (s + 1) * rows]
                pair[1, s, :, at] = mixed[s * rows : (s + 1) * rows, part]


def two_heads(block, scale):
    lane = lax.broadcasted_iota(jnp.int32, block.shape, 1)
    scaled = block * jnp.asarray(scale, block.dtype)
    zero = jnp.zeros_like(block)
    return jnp.concatenate(
        [jnp.where(lane < HEAD_DIM, scaled, zero), jnp.where(lane < HEAD_DIM, zero, scaled)]
    )


def own_lanes(both):
    rows = both.shape[1] // 2
    lane = lax.broadcasted_iota(jnp.int32, (both.shape[0], rows), 0)
    return jnp.where(lane < HEAD_DIM, both[:, :rows], both[:, rows:]).T


def fill_bias(bias, starts, rank):
    rows = bias.shape[1]
    key = lax.broadcasted_iota(jnp.int32, (rows, rows), 0)
    place = rank * rows + lax.broadcasted_iota(jnp.int32, (rows, rows), 1)
    begin = starts[...]
    for t in range(4):
        x, c = lax.div(rank, 2), lax.rem(rank, 2)
        owner = (1 - x if t >= 2 else x) * 2 + (1 - c if t % 2 else c)
        at = owner * rows + key
        bias[t] = jnp.where((at >= begin) & (at <= place), 0.0, masked_score)


NT = (((1,), (1,)), ((), ()))
TN = (((0,), (0,)), ((), ()))


def attend_step(rank, begin, starts, q, tiles, out, log_total, bias, scores, peak, total, acc):
    f32, bf16 = jnp.float32, jnp.bfloat16

    @pl.when(begin)
    def _():
        fill_bias(bias, starts, rank)

    high = rank >= 2
    stacked = two_heads(q, score_scale)

    def score(t):
        s = lax.dot_general(tiles[t][0][...], stacked, NT, preferred_element_type=f32)
        s = s + jnp.concatenate([bias[t], bias[t]], axis=1)
        scores[t] = s
        return jnp.max(s, axis=0, keepdims=True)

    def gather_values(t, top):
        e = jnp.exp(scores[t] - top)
        part = lax.dot_general(tiles[t][1][...], e.astype(bf16), TN, preferred_element_type=f32)
        return jnp.sum(e, axis=0, keepdims=True), part

    peak[...] = jnp.maximum(score(0), score(1))

    @pl.when(high)
    def _():
        peak[...] = jnp.maximum(peak[...], jnp.maximum(score(2), score(3)))

    top = peak[...]
    sum_a, acc_a = gather_values(0, top)
    sum_b, acc_b = gather_values(1, top)
    total[...] = sum_a + sum_b
    acc[...] = acc_a + acc_b

    @pl.when(high)
    def _():
        top = peak[...]
        sum_a, acc_a = gather_values(2, top)
        sum_b, acc_b = gather_values(3, top)
        total[...] += sum_a + sum_b
        acc[...] += acc_a + acc_b

    out[...] = own_lanes(acc[...] / total[...]).astype(bf16)
    log_total[...] = peak[...] + jnp.log(total[...])


def attend_scratch(rows):
    return [
        pltpu.VMEM((4, rows, rows), jnp.float32),
        pltpu.VMEM((4, rows, 2 * rows), jnp.float32),
        pltpu.VMEM((1, 2 * rows), jnp.float32),
        pltpu.VMEM((1, 2 * rows), jnp.float32),
        pltpu.VMEM((128, 2 * rows), jnp.float32),
    ]


def attend_back_step(
    rank, begin, starts, q, tiles, context, d_context, log_total, cos_t, sin_t, d_q, d_tiles, bias, acc
):
    f32, bf16 = jnp.float32, jnp.bfloat16

    @pl.when(begin)
    def _():
        fill_bias(bias, starts, rank)

    high = rank >= 2
    stacked = two_heads(q, score_scale)
    stacked_do = two_heads(d_context, 1.0)
    turned_product = (d_context.astype(f32) * context.astype(f32)).T
    delta = jnp.concatenate(
        [
            jnp.sum(turned_product[:HEAD_DIM], axis=0, keepdims=True),
            jnp.sum(turned_product[HEAD_DIM:], axis=0, keepdims=True),
        ],
        axis=1,
    )
    lse = log_total[...]

    def one(t):
        keys, values = tiles[t][0][...], tiles[t][1][...]
        s = lax.dot_general(keys, stacked, NT, preferred_element_type=f32)
        s = s + jnp.concatenate([bias[t], bias[t]], axis=1)
        p = jnp.exp(s - lse)
        dp = lax.dot_general(values, stacked_do, NT, preferred_element_type=f32)
        ds = (p * (dp - delta)).astype(bf16)
        d_tiles[t][1][...] = jnp.dot(p.astype(bf16), stacked_do, preferred_element_type=f32).astype(bf16)
        d_tiles[t][0][...] = jnp.dot(ds, stacked, preferred_element_type=f32).astype(bf16)
        return lax.dot_general(keys, ds, TN, preferred_element_type=f32)

    acc[...] = one(0) + one(1)

    @pl.when(high)
    def _():
        acc[...] += one(2) + one(3)

    d_q[...] = turned(own_lanes(acc[...]) * score_scale, cos_t[...], sin_t[...], -1.0).astype(bf16)


def attend_back_scratch(rows):
    return [pltpu.VMEM((4, rows, rows), jnp.float32), pltpu.VMEM((128, 2 * rows), jnp.float32)]


def position():
    dp = lax.axis_index("dp")
    ct = lax.axis_index("ctx")
    return lax.div(dp, 2), lax.rem(dp, 2), lax.div(ct, 2), lax.rem(ct, 2)


def visit(step, z, planes):
    back = planes - 1 - step
    high = back + jnp.where(back >= z, 1, 0)
    low = planes - 1 - back
    low = low - jnp.where(low <= z, 1, 0)
    other = jnp.where(z < planes // 2, low, high)
    return jnp.where(step == 0, z, other)


def device(z, y, x, c):
    return (z * 2 + y, x * 2 + c)


def halves(shape):
    if shape[0] % 2 == 0:
        cut = shape[0] // 2
        return (pl.ds(0, cut), slice(None), slice(None)), (pl.ds(cut, cut), slice(None), slice(None))
    cut = shape[2] // 2 // 128 * 128
    return (
        (slice(None), slice(None), pl.ds(0, cut)),
        (slice(None), slice(None), pl.ds(cut, shape[2] - cut)),
    )


def entry_barrier(z, y, x, c, planes):
    barrier = pltpu.get_barrier_semaphore()

    def hello(target):
        pl.semaphore_signal(barrier, inc=1, device_id=target, device_id_type=MESH_ID)

    hello(device(z, y, 1 - x, c))
    hello(device(z, 1 - y, x, c))
    hello(device(z, y, x, 1 - c))

    @pl.when(z > 0)
    def _():
        hello(device(z - 1, y, x, c))

    @pl.when(z < planes - 1)
    def _():
        hello(device(z + 1, y, x, c))

    pl.semaphore_wait(barrier, 3 + jnp.where(z > 0, 1, 0) + jnp.where(z < planes - 1, 1, 0))


def forward_kernel(planes, shapes, first_group, *refs):
    n = len(shapes)
    ins, refs = refs[:n], refs[n:]
    tok, first, starts, cos_table, sin_table = refs[:5]
    outs, refs = refs[5 : 5 + n], refs[5 + n :]
    normed, query, mine, near, chip, far, context, log_total = refs[:8]
    sems, refs = refs[8:19], refs[19:]
    own_sem, z_send, z_recv, x_send, x_recv, y_send, y_recv, d_send, d_recv, c_send, c_recv = sems
    tile_send, tile_recv, load_sem, gains, *weights = refs[: 4 + first_group - 1]
    scratch = refs[4 + first_group - 1 :]
    z, y, x, c = position()
    entry_barrier(z, y, x, c, planes)
    local = [
        pltpu.make_async_copy(ins[g], outs[g].at[:, z, y, x, c], own_sem.at[g]) for g in range(n)
    ]
    for copy in local:
        copy.start()

    def push(src, dst, send, recv, target):
        return pltpu.make_async_remote_copy(
            src_ref=src,
            dst_ref=dst,
            send_sem=send,
            recv_sem=recv,
            device_id=target,
            device_id_type=MESH_ID,
        )

    def spot(g, zz, yy, xx):
        return outs[g].at[:, zz, yy, xx, c]

    def z_copy(g, zz, up, own):
        side = 1 if up else 0
        return push(
            ins[g] if own else spot(g, zz, y, x),
            spot(g, zz, y, x),
            z_send.at[g, zz, side],
            z_recv.at[g, zz],
            device(z + 1 if up else z - 1, y, x, c),
        )

    def x_copy(g, zz, own):
        return push(
            ins[g] if own else spot(g, zz, y, x),
            spot(g, zz, y, x),
            x_send.at[g, zz],
            x_recv.at[g, zz],
            device(z, y, 1 - x, c),
        )

    def y_copy(g, zz, own):
        return push(
            ins[g] if own else spot(g, zz, y, x),
            spot(g, zz, y, x),
            y_send.at[g, zz],
            y_recv.at[g, zz],
            device(z, 1 - y, x, c),
        )

    def relay(g, zz, half, by_y):
        here = spot(g, zz, y, 1 - x) if by_y else spot(g, zz, 1 - y, x)
        here = here.at[halves(shapes[g])[half]]
        return push(
            here,
            here,
            d_send.at[g, zz, 2 * half if by_y else 1],
            d_recv.at[g, zz, half],
            device(z, 1 - y, x, c) if by_y else device(z, y, 1 - x, c),
        )

    def diag_arrival(g, zz, half):
        here = spot(g, zz, 1 - y, 1 - x).at[halves(shapes[g])[half]]
        return push(
            here, here, d_send.at[g, zz, half], d_recv.at[g, zz, half], device(z, y, x, 1 - c)
        )

    def core_copy(g, zz, mine):
        here = outs[g].at[:, zz, :, :, c if mine else 1 - c]
        return push(here, here, c_send.at[g, zz], c_recv.at[g, zz], device(z, y, x, 1 - c))

    def on_links(g, t, act):
        zz = visit(t, z, planes)

        def both(own):
            up = (z < planes - 1) if own else (zz < z) & (z < planes - 1)
            down = (z > 0) if own else (zz > z) & (z > 0)
            pl.when(down)(lambda: act(z_copy(g, zz, False, own)))
            pl.when(up)(lambda: act(z_copy(g, zz, True, own)))
            act(x_copy(g, zz, own))
            act(y_copy(g, zz, own))

        pl.when(t == 0)(lambda: both(True))
        pl.when(t > 0)(lambda: both(False))

    def on_relays(g, t, act, between=lambda: None):
        zz = visit(t, z, planes)
        act(relay(g, zz, 0, True))
        if g < first_group:
            between()
            act(relay(g, zz, 1, False))
            return
        lean = t > 0
        pl.when(lean & (x == 1))(lambda: act(relay(g, zz, 1, True)))
        between()
        pl.when((x == 1) | jnp.logical_not(lean))(lambda: act(relay(g, zz, 1, False)))

    def start(copy):
        copy.start()

    def wait_send(copy):
        copy.wait_send()

    def stage_line(g, t):
        @pl.when(t > 0)
        def _():
            z_copy(g, visit(t, z, planes), True, False).wait_recv()

        on_links(g, t, start)

    def stage_plane(g, t):
        zz = visit(t, z, planes)
        x_copy(g, zz, False).wait_recv()
        on_relays(g, t, start, lambda: y_copy(g, zz, False).wait_recv())

    def stage_core(g, t):
        zz = visit(t, z, planes)
        pl.when(t == 0)(lambda: local[g].wait())
        diag_arrival(g, zz, 0).wait_recv()
        diag_arrival(g, zz, 1).wait_recv()
        core_copy(g, zz, True).start()

    seqs, rows, width = query.shape
    pairs = width // 128
    partner = device(z, y, x, 1 - c)

    def to_partner(s):
        return push(
            mine.at[:, s], near.at[:, s], tile_send.at[0, s], tile_recv.at[0, s], partner
        )

    def to_x(s):
        return push(
            mine.at[:, s],
            chip.at[:, s],
            tile_send.at[1, s],
            tile_recv.at[1, s],
            device(z, y, 1 - x, c),
        )

    def passed_on(s):
        return push(
            chip.at[:, s], far.at[:, s], tile_send.at[2, s], tile_recv.at[2, s], partner
        )

    def send_tiles(s):
        to_partner(s).start()
        pl.when(x == 0)(lambda: to_x(s).start())

    def projection():
        @pl.loop(0, planes)
        def _(t):
            for g in range(first_group):
                core_copy(g, visit(t, z, planes), False).wait_recv()

        loads = [
            pltpu.make_async_copy(outs[g].at[0], buf, load_sem.at[g])
            for g, buf in enumerate([gains, *weights])
        ]
        for copy in loads:
            copy.start()
        loads[0].wait()
        flat_gains = [gains[i, j, k, m] for i in range(planes) for j in (0, 1) for k in (0, 1) for m in (0, 1)]
        per = len(flat_gains) * 128 // width
        gain = jnp.concatenate(
            [
                sum(b[:1].astype(jnp.float32) for b in flat_gains[i * per : (i + 1) * per])
                for i in range(width // 128)
            ],
            axis=1,
        )
        normalise(tok, gain, normed)
        for copy in loads[1:]:
            copy.wait()
        as_blocks = lambda w: w.reshape((planes * 8, *w.shape[4:]))
        project(
            normed, first, *[as_blocks(w) for w in weights], cos_table, sin_table, query, mine
        )
        for s in range(seqs):
            send_tiles(s)

    def unit(s, p):
        lanes = pl.ds(pl.multiple_of(p * 128, 128), 128)
        attend_step(
            lax.axis_index("ctx"),
            p == 0,
            starts.at[s],
            query[s, :, lanes],
            [[w.at[0, s, :, lanes], w.at[1, s, :, lanes]] for w in (mine, near, chip, far)],
            context.at[s, :, lanes],
            log_total.at[s, p],
            *scratch,
        )

    def attention():
        @pl.loop(0, seqs)
        def _(s):
            to_partner(s).wait_recv()

            @pl.when(x == 1)
            def _():
                to_x(s).wait_recv()
                passed_on(s).start()
                passed_on(s).wait_recv()

            @pl.loop(0, pairs)
            def _(p):
                unit(s, p)

    groups = (range(first_group), range(first_group, n))

    @pl.loop(0, 2 * planes + 2)
    def _(r):
        for stage, lag in ((stage_line, 0), (stage_plane, 1), (stage_core, 2)):
            for k, group in enumerate(groups):
                t = r - k * planes - lag
                for g in group:
                    pl.when((t >= 0) & (t < planes))(lambda: stage(g, t))
            if lag == 0:
                pl.when(r == planes + 3)(attention)
        pl.when(r == planes + 1)(projection)

    @pl.loop(0, planes)
    def _(t):
        zz = visit(t, z, planes)
        for g in range(n):
            if g >= first_group:
                core_copy(g, zz, False).wait_recv()
            core_copy(g, zz, True).wait_send()
            on_links(g, t, wait_send)
            on_relays(g, t, wait_send)

    for s in range(seqs):
        to_partner(s).wait_send()
        pl.when(x == 0)(lambda: to_x(s).wait_send())
        pl.when(x == 1)(lambda: passed_on(s).wait_send())


def forward(planes, first_group, blocks, tok, first, starts, cos_table, sin_table):
    blocks = [b[None] for b in blocks]
    n = len(blocks)
    shapes = [b.shape for b in blocks]
    seqs, _, rows = starts.shape
    width = tok.shape[1]
    bf16 = jnp.bfloat16
    dma = pltpu.SemaphoreType.DMA
    anywhere = pl.BlockSpec(memory_space=pl.ANY)
    vmem = pl.BlockSpec(memory_space=pltpu.VMEM)
    local = jax.ShapeDtypeStruct((seqs, rows, width), bf16)
    tile = jax.ShapeDtypeStruct((2, seqs, rows, width), bf16)
    got = pl.pallas_call(
        functools.partial(forward_kernel, planes, shapes, first_group),
        out_shape=[
            jax.ShapeDtypeStruct((s[0], planes, 2, 2, 2, s[1], s[2]), b.dtype)
            for s, b in zip(shapes, blocks)
        ]
        + [jax.ShapeDtypeStruct(tok.shape, bf16), local, *[tile] * 4, local]
        + [jax.ShapeDtypeStruct((seqs, width // 128, 1, 2 * rows), jnp.float32)],
        in_specs=[anywhere] * n + [vmem] * 5,
        out_specs=[anywhere] * n + [vmem] * 8,
        scratch_shapes=[
            dma((n,)),
            dma((n, planes, 2)),
            dma((n, planes)),
            dma((n, planes)),
            dma((n, planes)),
            dma((n, planes)),
            dma((n, planes)),
            dma((n, planes, 3)),
            dma((n, planes, 2)),
            dma((n, planes)),
            dma((n, planes)),
            dma((3, seqs)),
            dma((3, seqs)),
            dma((first_group,)),
            *[pltpu.VMEM((planes, 2, 2, 2, *s[1:]), bf16) for s in shapes[:first_group]],
            *attend_scratch(rows),
        ],
        compiler_params=pltpu.CompilerParams(
            collective_id=0, has_side_effects=True, vmem_limit_bytes=67043328
        ),
        name="forward",
    )(*blocks, tok, first, starts, cos_table, sin_table)
    full = [g.reshape(planes * 8 * s[1], s[2]) for g, s in zip(got, shapes)]
    return full, got[n:]


def columns(shape, half):
    cut = shape[1] // 2 // 128 * 128
    return pl.ds(0, cut) if half == 0 else pl.ds(cut, shape[1] - cut)


class Reduction:
    def __init__(self, **steps):
        self.__dict__.update(steps)


def reduction(planes, shapes, routed, own_at, away_at, before_core, boxes, sems, outs):
    n = len(shapes)
    from_core, from_dx, from_dy, from_x, from_y, from_z = (
        boxes[k * n : (k + 1) * n] for k in range(6)
    )
    c_send, c_recv, d_send, d_recv, x_send, x_recv, y_send, y_recv, z_send, z_recv = sems
    z, y, x, c = position()

    def push(src, dst, send, recv, target):
        return pltpu.make_async_remote_copy(
            src_ref=src,
            dst_ref=dst,
            send_sem=send,
            recv_sem=recv,
            device_id=target,
            device_id_type=MESH_ID,
        )

    f32 = jnp.float32

    def add(dst, *srcs):
        total = dst[...].astype(f32)
        for src in srcs:
            total = total + src[...].astype(f32)
        dst[...] = total.astype(dst.dtype)

    def core_copy(g, zz):
        return push(
            away_at(g, zz),
            from_core[g].at[zz],
            c_send.at[g, zz],
            c_recv.at[g, zz],
            device(z, y, x, 1 - c),
        )

    def diag_x(g, zz):
        return push(
            own_at(g, zz, 1 - y, 1 - x).at[:, columns(shapes[g], 0)],
            from_dx[g].at[zz],
            d_send.at[g, zz, 0],
            d_recv.at[g, zz, 0],
            device(z, y, 1 - x, c),
        )

    def diag_y(g, zz, full):
        part = slice(None) if full else columns(shapes[g], 1)
        return push(
            own_at(g, zz, 1 - y, 1 - x).at[:, part],
            from_dy[g].at[zz, :, part],
            d_send.at[g, zz, 1],
            d_recv.at[g, zz, 1],
            device(z, 1 - y, x, c),
        )

    def x_copy(g, zz):
        return push(
            own_at(g, zz, y, 1 - x),
            from_x[g].at[zz],
            x_send.at[g, zz],
            x_recv.at[g, zz],
            device(z, y, 1 - x, c),
        )

    def y_copy(g, zz):
        return push(
            own_at(g, zz, 1 - y, x),
            from_y[g].at[zz],
            y_send.at[g, zz],
            y_recv.at[g, zz],
            device(z, 1 - y, x, c),
        )

    def z_copy(g, zz, up):
        slot = zz if up else jnp.where(zz == z - 1, planes, zz)
        return push(
            own_at(g, zz, y, x),
            from_z[g].at[slot],
            z_send.at[g, zz],
            z_recv.at[g, slot],
            device(z + 1 if up else z - 1, y, x, c),
        )

    def z_arrival(g, slot):
        return push(
            from_z[g].at[slot],
            from_z[g].at[slot],
            z_send.at[g, 0],
            z_recv.at[g, slot],
            device(z, y, x, 1 - c),
        )

    def lean_or_even(t, lean, even):
        if not routed:
            even()
            return
        is_lean = (x == 1) & (t < planes - 2)
        pl.when(jnp.logical_not(is_lean))(even)
        pl.when(is_lean)(lean)

    def stage_core(g, t):
        zz = visit(t, z, planes)
        before_core(g, zz)
        core_copy(g, zz).wait_recv()
        add(own_at(g, zz, 1 - y, 1 - x), from_core[g].at[zz, 1 - y, 1 - x])

        def even():
            diag_x(g, zz).start()
            diag_y(g, zz, False).start()

        lean_or_even(t, lambda: diag_y(g, zz, True).start(), even)
        add(own_at(g, zz, 1 - y, x), from_core[g].at[zz, 1 - y, x])
        if routed:

            @pl.when((x == 0) & (t < planes - 2))
            def _():
                y_copy(g, zz).start()

        add(own_at(g, zz, y, 1 - x), from_core[g].at[zz, y, 1 - x])
        add(own_at(g, zz, y, x), from_core[g].at[zz, y, x])

    def stage_plane(g, t):
        zz = visit(t, z, planes)

        def take_x():
            diag_x(g, zz).wait_recv()
            add(own_at(g, zz, 1 - y, x).at[:, columns(shapes[g], 0)], from_dx[g].at[zz])
            y_copy(g, zz).start()

        def take_y(full):
            part = slice(None) if full else columns(shapes[g], 1)
            diag_y(g, zz, full).wait_recv()
            add(own_at(g, zz, y, 1 - x).at[:, part], from_dy[g].at[zz, :, part])
            x_copy(g, zz).start()

        if not routed:
            take_x()
            take_y(False)
            return
        lean = t < planes - 2
        pl.when((x == 1) | jnp.logical_not(lean))(take_x)
        pl.when((x == 1) & lean)(lambda: take_y(True))
        pl.when((x == 0) | jnp.logical_not(lean))(lambda: take_y(False))

    def stage_line(g, t):
        zz = visit(t, z, planes)
        x_copy(g, zz).wait_recv()
        y_copy(g, zz).wait_recv()
        here = own_at(g, zz, y, x)

        @pl.when(t > 0)
        def _():
            add(here, from_x[g].at[zz], from_y[g].at[zz])
            farther = jnp.where(zz > z, z > 0, z < planes - 1)

            @pl.when(farther)
            def _():
                z_arrival(g, zz).wait_recv()
                add(here, from_z[g].at[zz])

            @pl.when(zz > z)
            def _():
                z_copy(g, zz, True).start()

            @pl.when(zz < z)
            def _():
                z_copy(g, zz, False).start()

        @pl.when(t == 0)
        def _():
            outs[g][...] = (
                here[...].astype(f32)
                + from_x[g][zz].astype(f32)
                + from_y[g][zz].astype(f32)
            )

            @pl.when(z > 0)
            def _():
                z_arrival(g, zz).wait_recv()
                outs[g][...] += from_z[g][zz].astype(f32)

            @pl.when(z < planes - 1)
            def _():
                z_arrival(g, planes).wait_recv()
                outs[g][...] += from_z[g][planes].astype(f32)

    def stage_end(g, t):
        zz = visit(t, z, planes)
        core_copy(g, zz).wait_send()

        def even():
            diag_x(g, zz).wait_send()
            diag_y(g, zz, False).wait_send()

        lean_or_even(t, lambda: diag_y(g, zz, True).wait_send(), even)
        x_copy(g, zz).wait_send()
        y_copy(g, zz).wait_send()

        @pl.when(t > 0)
        def _():
            z_copy(g, zz, True).wait_send()

    return Reduction(
        core_copy=core_copy, core=stage_core, plane=stage_plane, line=stage_line, end=stage_end
    )


def remote(src, dst, send, recv, target):
    return pltpu.make_async_remote_copy(
        src_ref=src,
        dst_ref=dst,
        send_sem=send,
        recv_sem=recv,
        device_id=target,
        device_id_type=MESH_ID,
    )


def scatter_kernel(planes, shapes, *refs):
    n = len(shapes)
    parts, refs = refs[:n], refs[n:]
    starts, query, *tiles, context, d_context, log_total, cos_table, sin_table = refs[:11]
    refs = refs[11:]
    outs, refs = refs[:n], refs[n:]
    d_query, d_key, d_value, first_grad = refs[:4]
    refs = refs[4:]
    mine, near, chip, far, from_b, from_d, tile_send, tile_recv, bias, acc = refs[-10:]
    own, boxes, own_sem, sems = refs[:n], refs[n : 7 * n], refs[7 * n], refs[7 * n + 1 : -10]
    z, y, x, c = position()
    entry_barrier(z, y, x, c, planes)
    f32 = jnp.float32
    push = remote

    def add(dst, src):
        dst[...] = (dst[...].astype(f32) + src[...].astype(f32)).astype(dst.dtype)

    def load(g, zz):
        return pltpu.make_async_copy(
            parts[g].at[zz, :, :, c], own[g].at[zz], own_sem.at[g, zz]
        )

    steps = reduction(
        planes,
        shapes,
        True,
        lambda g, zz, yy, xx: own[g].at[zz, yy, xx],
        lambda g, zz: parts[g].at[zz, :, :, 1 - c],
        lambda g, zz: load(g, zz).wait(),
        boxes,
        sems,
        outs,
    )

    partner = device(z, y, x, 1 - c)
    seqs, rows = mine.shape[1:3]
    pairs = mine.shape[3] // 128

    def send_b(s):
        return push(
            near.at[:, s], from_b.at[:, s], tile_send.at[0, s], tile_recv.at[0, s], partner
        )

    def send_d(s):
        return push(
            far.at[:, s], from_d.at[:, s], tile_send.at[1, s], tile_recv.at[1, s], partner
        )

    def send_back(s):
        return push(
            chip.at[:, s],
            chip.at[:, s],
            tile_send.at[2, s],
            tile_recv.at[2, s],
            device(z, y, 1 - x, c),
        )

    def unit(s, p):
        lanes = pl.ds(pl.multiple_of(p * 128, 128), 128)
        flat = pl.ds(pl.multiple_of(s * rows, rows), rows)
        two = lambda ref: [ref.at[0, s, :, lanes], ref.at[1, s, :, lanes]]
        attend_back_step(
            lax.axis_index("ctx"),
            p == 0,
            starts.at[s],
            query[s, :, lanes],
            [two(t) for t in tiles],
            context[s, :, lanes],
            d_context[s, :, lanes],
            log_total.at[s, p],
            cos_table.at[flat],
            sin_table.at[flat],
            d_query.at[s, :, lanes],
            [two(t) for t in (mine, near, chip, far)],
            bias,
            acc,
        )

    def work(i):
        @pl.when((i >= 2) & (i <= 2 * seqs) & (lax.rem(i, 2) == 0) & (x == 1))
        def _():
            s = lax.div(i, 2) - 1
            send_d(s).wait_recv()

            @pl.loop(0, 2 * rows // 32)
            def _(j):
                kind = lax.div(j, rows // 32)
                at = pl.ds(pl.multiple_of(lax.rem(j, rows // 32) * 32, 32), 32)
                add(chip.at[kind, s, at], from_d.at[kind, s, at])

            send_back(s).start()

        @pl.when((i >= 0) & (i < 2 * seqs))
        def _():
            s = lax.div(i, 2)

            @pl.loop(0, pairs // 2)
            def _(p):
                unit(s, lax.rem(i, 2) * (pairs // 2) + p)

            @pl.when(lax.rem(i, 2) == 1)
            def _():
                send_b(s).start()
                pl.when(x == 1)(lambda: send_d(s).start())

    @pl.loop(0, planes)
    def _(r):
        zz = visit(planes - 1 - r, z, planes)
        for g in range(n):
            steps.core_copy(g, zz).start()
            load(g, zz).start()

    @pl.loop(0, planes + 2)
    def _(r):
        t = planes - 1 - r
        for g in range(n):
            pl.when(r < planes)(lambda: steps.core(g, t))
        for g in range(n):
            if g == 0:
                work(2 * r - 2)
            pl.when((r >= 1) & (r < planes + 1))(lambda: steps.plane(g, t + 1))
        work(2 * r - 1)
        for g in range(n):
            pl.when(r >= 2)(lambda: steps.line(g, t + 2))

    @pl.loop(0, planes)
    def _(t):
        for g in range(n):
            steps.end(g, t)

    for s in range(seqs):
        send_b(s).wait()

        @pl.when(x == 0)
        def _():
            send_back(s).wait_recv()

        @pl.when(x == 1)
        def _():
            send_d(s).wait_send()
            send_back(s).wait_send()

    @pl.when(x == 1)
    def _():
        chip[...] = jnp.zeros_like(chip)

    @pl.loop(0, seqs * rows // 32)
    def _(i):
        seq = lax.div(i, rows // 32)
        at = pl.ds(pl.multiple_of(lax.rem(i, rows // 32) * 32, 32), 32)
        flat = pl.ds(pl.multiple_of(i * 32, 32), 32)
        cos_rows, sin_rows = cos_table[flat, :], sin_table[flat, :]
        for k in range(pairs):
            lanes = pl.ds(k * 128, 128)

            def summed(kind):
                return (
                    mine[kind, seq, at, lanes].astype(f32)
                    + from_b[kind, seq, at, lanes].astype(f32)
                    + chip[kind, seq, at, lanes].astype(f32)
                )

            d_key[flat, lanes] = turned(summed(0), cos_rows, sin_rows, -1.0).astype(jnp.bfloat16)
            half = 0.5 * summed(1)
            d_value[flat, lanes] = half.astype(jnp.bfloat16)
            first_grad[flat, lanes] = half


def boxes_of(planes, shapes, types):
    def boxes(lead, narrow=False):
        out = []
        for s, d in zip(shapes, types):
            width = s[1] // 2 // 128 * 128 if narrow else s[1]
            out.append(pltpu.VMEM((*lead, s[0], width), d))
        return out

    return [
        *boxes((planes, 2, 2)),
        *boxes((planes,), True),
        *boxes((planes,)),
        *boxes((planes,)),
        *boxes((planes,)),
        *boxes((planes + 1,)),
    ]


def sems_of(planes, n):
    dma = pltpu.SemaphoreType.DMA
    return [
        dma((n, planes)),
        dma((n, planes)),
        dma((n, planes, 2)),
        dma((n, planes, 2)),
        dma((n, planes)),
        dma((n, planes)),
        dma((n, planes)),
        dma((n, planes)),
        dma((n, planes)),
        dma((n, planes + 1)),
    ]


def scatter_sum(planes, partials, attention):
    n = len(partials)
    partials = [
        p.reshape(planes, 2, 2, 2, p.shape[0] // (planes * 8), p.shape[1]) for p in partials
    ]
    shapes = [p.shape[4:] for p in partials]
    bf16 = jnp.bfloat16
    dma = pltpu.SemaphoreType.DMA
    box = attention[2].shape
    seqs, rows, width = box[1:]
    flat = (seqs * rows, width)
    vmem = pl.BlockSpec(memory_space=pltpu.VMEM)
    return pl.pallas_call(
        functools.partial(scatter_kernel, planes, shapes),
        out_shape=[jax.ShapeDtypeStruct(s, jnp.float32) for s in shapes]
        + [
            jax.ShapeDtypeStruct(box[1:], bf16),
            jax.ShapeDtypeStruct(flat, bf16),
            jax.ShapeDtypeStruct(flat, bf16),
            jax.ShapeDtypeStruct(flat, jnp.float32),
        ],
        in_specs=[pl.BlockSpec(memory_space=pl.ANY)] * n + [vmem] * len(attention),
        out_specs=[vmem] * (n + 4),
        scratch_shapes=[
            *[pltpu.VMEM((planes, 2, 2, *s), bf16) for s in shapes],
            *boxes_of(planes, shapes, [bf16] * n),
            dma((n, planes)),
            *sems_of(planes, n),
            *[pltpu.VMEM(box, bf16)] * 6,
            dma((3, seqs)),
            dma((3, seqs)),
            *attend_back_scratch(rows),
        ],
        compiler_params=pltpu.CompilerParams(
            collective_id=1, has_side_effects=True, vmem_limit_bytes=67043328
        ),
        name="gradient_scatter",
    )(*partials, *attention)


def last_kernel(planes, shapes, *refs):
    f32, bf16 = jnp.float32, jnp.bfloat16
    n = len(shapes)
    normed, *d_proj = refs[:4]
    w_in, tok_in, d_residual_in, attn_gain, d_ffn_gain = refs[4:7], *refs[7:11]
    outs, token_grad = refs[11 : 11 + n], refs[11 + n]
    refs = refs[12 + n :]
    weights, tok, d_residual, gain_sum = refs[:3], *refs[3:6]
    parts, boxes, sems, load_sem = refs[6 : 6 + n], refs[6 + n : 6 + 7 * n], refs[6 + 7 * n : -1], refs[-1]
    z, y, x, c = position()
    loads = [
        pltpu.make_async_copy(src, dst, load_sem.at[i])
        for i, (src, dst) in enumerate(zip([*w_in, tok_in, d_residual_in], [*weights, tok, d_residual]))
    ]
    for copy in loads:
        copy.start()
    entry_barrier(z, y, x, c, planes)
    rows, width = tok.shape
    steps = reduction(
        planes,
        shapes,
        False,
        lambda g, zz, yy, xx: parts[g].at[zz, yy, xx, c],
        lambda g, zz: parts[g].at[zz, :, :, 1 - c],
        lambda g, zz: None,
        boxes,
        sems,
        outs,
    )
    at_once = planes * 256 // width

    def weight_grads(j):
        lanes = pl.ds(pl.multiple_of(j * 256, 256), 256)
        for g in range(3):
            part = lax.dot_general(normed[:, lanes], d_proj[g][...], TN, preferred_element_type=f32)
            shape = (at_once, 2, 2, 2, *shapes[g])
            parts[g][pl.ds(j * at_once, at_once)] = part.reshape(shape).astype(bf16)

    def normed_grad():
        for copy in loads:
            copy.wait()

        @pl.loop(0, width // 256)
        def _(j):
            at = pl.ds(pl.multiple_of(j * 256, 256), 256)
            total = 0.0
            for g in range(3):
                total = total + lax.dot_general(
                    d_proj[g][...], weights[g][at, :], NT, preferred_element_type=f32
                )
            token_grad[:, at] = total

    def token_gradient():
        gain_sum[...] = jnp.zeros_like(gain_sum)

        @pl.loop(0, rows // 64)
        def _(i):
            at = pl.ds(pl.multiple_of(i * 64, 64), 64)
            values = tok[at, :].astype(f32)
            scale = inverse_rms(values)
            d_normed = token_grad[at, :]
            products = d_normed * values * scale
            gain_sum[...] += jnp.sum(products.reshape(8, 8, width), axis=0)
            weighted = d_normed * attn_gain[...]
            token_grad[at, :] = (
                d_residual[at, :]
                + scale * weighted
                - values * (scale * scale * scale) * jnp.mean(weighted * values, axis=-1, keepdims=True)
            )

        both = jnp.concatenate(
            [jnp.sum(gain_sum[...], axis=0, keepdims=True), d_ffn_gain[...], jnp.zeros((6, width), f32)]
        )
        per = planes * 8 * 256 // width
        for i in range(planes * 8):
            at = i // per * 256
            parts[3][i // 8, i // 4 % 2, i // 2 % 2, i % 2] = both[:, at : at + 256]

    def send_cores(g, t):
        steps.core_copy(g, visit(t, z, planes)).start()

    if at_once > 1:
        pl.loop(0, width // 256)(weight_grads)
    lag = 2

    @pl.loop(0, planes + 3 + lag)
    def _(r):
        t = planes - 1 - r

        @pl.when(r < planes)
        def _():
            if at_once == 1:
                weight_grads(visit(t, z, planes))
            for g in range(3):
                send_cores(g, t)

        for group, late in ((range(3), 0), ((3,), lag)):
            for step, behind in ((steps.core, 1), (steps.plane, 2), (steps.line, 3)):
                behind += late
                for g in group:
                    pl.when((r >= behind) & (r < planes + behind))(lambda: step(g, t + behind))

        @pl.when(r == 1)
        def _():
            normed_grad()

        @pl.when(r == 2)
        def _():
            token_gradient()

            @pl.loop(0, planes)
            def _(i):
                send_cores(3, i)

    @pl.loop(0, planes)
    def _(t):
        for g in range(n):
            steps.end(g, t)


def last(planes, normed, d_proj, weights, tok, d_residual, attn_gain, d_ffn_gain):
    f32, bf16 = jnp.float32, jnp.bfloat16
    width = tok.shape[1]
    shapes = [(width // (planes * 8), width)] * 3 + [(8, 256)]
    types = [bf16] * 3 + [f32]
    n = len(shapes)
    vmem, anywhere = pl.BlockSpec(memory_space=pltpu.VMEM), pl.BlockSpec(memory_space=pl.ANY)
    return pl.pallas_call(
        functools.partial(last_kernel, planes, shapes),
        out_shape=[jax.ShapeDtypeStruct(s, f32) for s in [*shapes, tok.shape]],
        in_specs=[vmem] * 4 + [anywhere] * 5 + [vmem] * 2,
        out_specs=[vmem] * (n + 1),
        scratch_shapes=[
            *[pltpu.VMEM((width, width), bf16)] * 3,
            pltpu.VMEM(tok.shape, bf16),
            pltpu.VMEM(tok.shape, f32),
            pltpu.VMEM((8, width), f32),
            *[pltpu.VMEM((planes, 2, 2, 2, *s), d) for s, d in zip(shapes, types)],
            *boxes_of(planes, shapes, types),
            *sems_of(planes, n),
            pltpu.SemaphoreType.DMA((5,)),
        ],
        compiler_params=pltpu.CompilerParams(
            collective_id=2, has_side_effects=True, vmem_limit_bytes=67043328
        ),
        name="last",
    )(normed, *d_proj, *weights, tok, d_residual, attn_gain, d_ffn_gain)


def on_device(
    planes,
    tokens,
    first_values,
    cotangent,
    segment_ids,
    attn_gain,
    w_query,
    w_key,
    w_value,
    w_out,
    ffn_gain,
    gate_weight,
    up_weight,
    down_weight,
):
    f32, bf16 = jnp.float32, jnp.bfloat16
    seqs, rows, width = tokens.shape
    rank = lax.axis_index("ctx")
    share = attn_gain.shape[0]
    per = 128 // share
    index = lax.axis_index("dp") * lax.axis_size("ctx") + rank
    place = lax.rem(index, per)
    here = jnp.arange(128, dtype=jnp.int32) // share == place
    spread = lambda gain: jnp.where(here, jnp.tile(gain, per), jnp.zeros((), bf16))
    gains = jnp.zeros((16, 128), bf16).at[0].set(spread(attn_gain)).at[1].set(spread(ffn_gain))
    starts, cos_table, sin_table = tables(segment_ids, rank, rows)
    flat = (seqs * rows, width)
    local = (seqs, rows, width)
    tokens = tokens.reshape(flat)
    mm = functools.partial(jnp.dot, preferred_element_type=f32)
    by_rows = lambda a, b: lax.dot_general(a, b, TN, preferred_element_type=f32).astype(bf16)
    back = lambda a, b: lax.dot_general(a, b, NT, preferred_element_type=f32)
    (gains, w_query, w_key, w_value, w_out, gate_weight, up_weight, down_weight), (
        normed_one,
        query_rot,
        *tiles,
        context3,
        log_total,
    ) = forward(
        planes,
        4,
        [gains, w_query, w_key, w_value, w_out, gate_weight, up_weight, down_weight],
        tokens,
        first_values.reshape(flat),
        starts,
        cos_table,
        sin_table,
    )
    gains = jnp.sum(gains.reshape(width // 128, per, 16, 128), axis=1)
    attn_gain = gains[:, 0].reshape(1, width)
    ffn_gain = gains[:, 1].reshape(1, width)
    context = context3.reshape(flat)
    tokens_float = tokens.astype(f32)
    cotangent = cotangent.reshape(flat)
    residual = tokens_float + mm(context, w_out)
    scale_two = inverse_rms(residual)
    second_normed = (residual * scale_two * ffn_gain.astype(f32)).astype(bf16)
    gate = mm(second_normed, gate_weight)
    up = mm(second_normed, up_weight)
    hidden = (swish(gate) * up).astype(bf16)
    output = (residual + mm(hidden, down_weight)).astype(bf16)

    out_float = cotangent.astype(f32)
    d_down = by_rows(hidden, cotangent)
    d_hidden = back(cotangent, down_weight)
    sigmoid_gate = jax.nn.sigmoid(gate)
    d_gate = (d_hidden * up * sigmoid_gate * (1.0 + gate * (1.0 - sigmoid_gate))).astype(bf16)
    d_up = (d_hidden * (gate * sigmoid_gate)).astype(bf16)
    d_gate_weight = by_rows(second_normed, d_gate)
    d_up_weight = by_rows(second_normed, d_up)
    d_normed_two = back(d_gate, gate_weight) + back(d_up, up_weight)
    d_ffn_gain = jnp.sum(d_normed_two * residual * scale_two, axis=0)
    weighted_two = d_normed_two * ffn_gain.astype(f32)
    d_residual = (
        out_float
        + scale_two * weighted_two
        - residual
        * (scale_two * scale_two * scale_two)
        * jnp.mean(weighted_two * residual, axis=-1, keepdims=True)
    )
    d_residual_low = d_residual.astype(bf16)
    d_out = by_rows(context, d_residual_low)
    d_context = back(d_residual_low, w_out).astype(bf16).reshape(local)
    s_down, s_gate, s_up, s_out, d_query, d_key, d_value, first_grad = scatter_sum(
        planes,
        [d_down, d_gate_weight, d_up_weight, d_out],
        [starts, query_rot, *tiles, context3, d_context, log_total, cos_table, sin_table],
    )
    d_query = d_query.reshape(flat)
    s_wq, s_wk, s_wv, s_gains, token_grad = last(
        planes,
        normed_one,
        [d_query, d_key, d_value],
        [w_query, w_key, w_value],
        tokens,
        d_residual,
        attn_gain.astype(f32),
        d_ffn_gain[None],
    )
    slot = lax.rem(index, 256 // share) * share
    s_gains = lax.dynamic_slice_in_dim(s_gains[:2], slot, share, 1)
    return (
        output.reshape(local),
        token_grad.reshape(local),
        first_grad.reshape(local),
        s_gains[0],
        s_wq,
        s_wk,
        s_wv,
        s_out,
        s_gains[1],
        s_gate,
        s_up,
        s_down,
    )


def solution(mesh):
    token, weight, vector = P("dp", "ctx", None), P(("dp", "ctx"), None), P(("dp", "ctx"))
    return jax.shard_map(
        functools.partial(on_device, mesh.shape["dp"] // 2),
        mesh=mesh,
        in_specs=(
            token,
            token,
            token,
            P("dp", None),
            vector,
            weight,
            weight,
            weight,
            weight,
            vector,
            weight,
            weight,
            weight,
        ),
        out_specs=(
            token,
            token,
            token,
            vector,
            weight,
            weight,
            weight,
            weight,
            vector,
            weight,
            weight,
            weight,
        ),
        check_vma=False,
    )
```

profile of v0, /device:TPU:0, one launch (start us, length us, event | category | flops | bytes accessed | tf_op | source)
XLA Modules:
  0.0 415.1 jit_solution(10432993672189395321)
XLA Ops:
  2.3 0.8 slice_compare_fusion
  4.9 1.8 fusion.7
  6.7 150.5 %forward.1 = (bf16[1,4,2,2,2,16,128]{6,5,4,3,2,1,0:T(8,128)(2,1)}, bf16[1,4,2,2,2,32,1024]{6,5,4,3,2,1,0:T(8,128)(2,1)}, bf16[1,4,2,2,2,32,1024]{6,5,4,3,2,1,0:T...) custom-call(bf16[1,16,128]{2,1,0:T(8,128)(2,1)} %copy-done.11, ...), custom_call_target="tpu_custom_call" | custom-call | tf_op jit(solution)/shard_map/forward/pallas_call | solution.py:541
  157.2 0.9 reduce_sum.42
  158.8 3.7 multiply_reduce_fusion.2
  162.8 4.9 %fusion.15 = f32[512,2816]{1,0:T(8,128)} fusion(bf16[512,1024]{1,0:T(8,128)(2,1)S(1)} %multiply_convert_fusion.1, bf16[1024,2816]{1,0:T(8,128)(2,1)S(1)} %bitcast.123), kind=kOutput, calls=%fused_computation.65 | convolution fusion | flops 2952790016 | bytes 12582912 | tf_op jit(solution)/shard_map/dot_general | solution.py:1256
  167.7 5.0 %fusion.14 = f32[512,2816]{1,0:T(8,128)} fusion(bf16[512,1024]{1,0:T(8,128)(2,1)S(1)} %multiply_convert_fusion.1, bf16[1024,2816]{1,0:T(8,128)(2,1)S(1)} %bitcast.127), kind=kOutput, calls=%fused_computation.64 | convolution fusion | flops 2952790016 | bytes 12582912 | tf_op jit(solution)/shard_map/dot_general | solution.py:1255
  172.7 9.9 %fusion.3 = (bf16[512,2816]{1,0:T(8,128)(2,1)S(1)}, bf16[512,2816]{1,0:T(8,128)(2,1)}, bf16[512,2816]{1,0:T(8,128)(2,1)}) fusion(f32[512,2816]{1,0:T(8,128)} %fusion.14, f32[512,2816]{1,0:T(8,128)} %fusion.15, bf16[2816,1024]{1,0:T(8,128)(2,1)S(1)} %bitcast.131, bf16[512,1024]{1,0:T(8,128)(2,1)S(1)} %bitcast.97), kind=kOutput, calls=%fused_computation.5 | convolution fusion | flops 2974416896 | bytes 27000832 | tf_op jit(solution)/shard_map/dot_general | solution.py:1229
  182.6 6.1 %add_convert_fusion = bf16[512,1024]{1,0:T(8,128)(2,1)} fusion(f32[512,1024]{1,0:T(8,128)S(1)} %get-tuple-element.110, bf16[512,2816]{1,0:T(8,128)(2,1)} %get-tuple-element.100, bf16[2816,1024]{1,0:T(8,128)(2,1)S(1)} %bitcast.132), kind=kOutput, calls=%fused_computation.15 | convolution fusion | flops 2953838592 | bytes 11796480 | tf_op jit(solution)/shard_map/dot_general | solution.py:1258
  188.7 3.2 fusion.16
  191.9 4.0 multiply_reduce_fusion
  196.5 1.0 copy-done.12
  197.5 2.3 convolution_convert_fusion.4
  199.9 2.6 convolution_convert_fusion.3
  202.5 5.1 %convolution_convert_fusion = bf16[1024,2816]{1,0:T(8,128)(2,1)} fusion(bf16[512,1024]{1,0:T(8,128)(2,1)S(1)} %multiply_convert_fusion.1, bf16[512,2816]{1,0:T(8,128)(2,1)S(1)} %get-tuple-element.98), kind=kOutput, calls=%fused_computation.9 | convolution fusion | flops 2955673600 | bytes 9699328 | tf_op jit(solution)/shard_map/dot_general | solution.py:1228
  207.6 5.1 %convolution_convert_fusion.1 = bf16[1024,2816]{1,0:T(8,128)(2,1)} fusion(bf16[512,1024]{1,0:T(8,128)(2,1)S(1)} %multiply_convert_fusion.1, bf16[512,2816]{1,0:T(8,128)(2,1)S(1)} %copy-done.15), kind=kOutput, calls=%fused_computation.10 | convolution fusion | flops 2955673600 | bytes 9699328 | tf_op jit(solution)/shard_map/dot_general | solution.py:1228
  212.6 5.0 %convolution_convert_fusion.2 = bf16[2816,1024]{1,0:T(8,128)(2,1)} fusion(bf16[512,2816]{1,0:T(8,128)(2,1)S(1)} %copy-done.13, bf16[512,1024]{1,0:T(8,128)(2,1)S(1)} %bitcast.98), kind=kOutput, calls=%fused_computation.11 | convolution fusion | flops 2955673600 | bytes 9699328 | tf_op jit(solution)/shard_map/dot_general | solution.py:1228
  217.6 139.7 %gradient_scatter.1 = (f32[88,1024]{1,0:T(8,128)}, f32[32,2816]{1,0:T(8,128)}, f32[32,2816]{1,0:T(8,128)}, f32[32,1024]{1,0:T(8,128)}, bf16[2,256,1024]{2,1,0:T(...) custom-call(bf16[4,2,2,2,88,1024]{5,4,3,2,1,0:T(8,128)(2,1)} %bitcast.87, ...), custom_call_target="tpu_custom_call" | custom-call | tf_op jit(solution)/shard_map/gradient_scatter/pallas_call | solution.py:1020
  357.3 47.0 %last.1 = (f32[32,1024]{1,0:T(8,128)}, f32[32,1024]{1,0:T(8,128)}, f32[32,1024]{1,0:T(8,128)}, f32[8,256]{1,0:T(8,128)}, f32[512,1024]{1,0:T(8,128)}) custom-call(bf16[512,1024]{1,0:T(8,128)(2,1)} %get-tuple-element.71.refs_0_, bf16[512,1024]{1,0:T(8,128)(2,1)} %bitcast.101, bf16[512,1024]{1,0:T(8,128)(2,1)} %get-tuple-element.79.refs_2_, ...), custom_call_target="tpu_custom_call" | custom-call | tf_op jit(solution)/shard_map/last/pallas_call | solution.py:1175
  404.3 0.8 slice.62
  405.7 3.2 copy.49
  408.9 1.3 copy.50
  412.9 0.7 copy.55
  413.6 0.7 copy.56
  (79 shorter events, 8.8 us)
Async XLA Ops:
  2.3 0.9 copy-start.11
  158.8 3.9 slice-start
  158.8 4.0 slice-start.1
  162.5 5.2 %slice-start.2 = ((s8[5767168]{0:T(1024)(128)(4,1)}), s8[4194304]{0:T(1024)(128)(4,1)S(1)}, s32[]{:S(2)}) async-start(s8[5767168]{0:T(1024)(128)(4,1)} %bitcast.125), calls=%async_computation.2 | async-start | bytes 8388608
  162.7 4.9 %slice-start.3 = ((s8[5767168]{0:T(1024)(128)(4,1)}), s8[1572864]{0:T(1024)(128)(4,1)S(1)}, s32[]{:S(2)}) async-start(s8[5767168]{0:T(1024)(128)(4,1)} %bitcast.125), calls=%async_computation.3 | async-start | bytes 3145728
  162.7 9.9 %slice-start.4 = ((s8[5767168]{0:T(1024)(128)(4,1)}), s8[4194304]{0:T(1024)(128)(4,1)S(1)}, s32[]{:S(2)}) async-start(s8[5767168]{0:T(1024)(128)(4,1)} %bitcast.129), calls=%async_computation.4 | async-start | bytes 8388608
  167.7 5.0 %copy-start.2 = (bf16[2,256,1024]{2,1,0:T(8,128)(2,1)S(1)}, bf16[2,256,1024]{2,1,0:T(8,128)(2,1)}, u32[]{:S(2)}) copy-start(bf16[2,256,1024]{2,1,0:T(8,128)(2,1)} %param.19) | copy-start | bytes 3145732
  167.7 5.0 %slice-start.5 = ((s8[5767168]{0:T(1024)(128)(4,1)}), s8[1572864]{0:T(1024)(128)(4,1)S(1)}, s32[]{:S(2)}) async-start(s8[5767168]{0:T(1024)(128)(4,1)} %bitcast.129), calls=%async_computation.5 | async-start | bytes 3145728
  182.6 6.1 %copy-start.14 = (bf16[512,2816]{1,0:T(8,128)(2,1)S(1)}, bf16[512,2816]{1,0:T(8,128)(2,1)}, u32[]{:S(2)}) copy-start(bf16[512,2816]{1,0:T(8,128)(2,1)} %get-tuple-element.99) | copy-start | bytes 8650756
  195.9 1.6 copy-start.12
  197.5 2.3 copy-start
  197.5 2.3 copy-start.3
  202.5 5.1 %copy-start.15 = (bf16[512,2816]{1,0:T(8,128)(2,1)S(1)}, bf16[512,2816]{1,0:T(8,128)(2,1)}, u32[]{:S(2)}) copy-start(bf16[512,2816]{1,0:T(8,128)(2,1)} %get-tuple-element.99) | copy-start | bytes 8650756
  207.6 5.1 %copy-start.13 = (bf16[512,2816]{1,0:T(8,128)(2,1)S(1)}, bf16[512,2816]{1,0:T(8,128)(2,1)}, u32[]{:S(2)}) copy-start(bf16[512,2816]{1,0:T(8,128)(2,1)} %get-tuple-element.100) | copy-start | bytes 8650756
  404.3 4.6 %copy-start.1 = (f32[512,1024]{1,0:T(8,128)S(1)}, f32[512,1024]{1,0:T(8,128)}, u32[]{:S(2)}) copy-start(f32[512,1024]{1,0:T(8,128)} %get-tuple-element.85) | copy-start | bytes 6291460
  408.9 1.4 copy-start.10
  408.9 2.0 copy-start.9
  408.9 2.7 copy-start.8
  408.9 3.3 copy-start.7
  408.9 4.0 copy-start.6
  408.9 4.7 %copy-start.5 = (f32[32,2816]{1,0:T(8,128)S(1)}, f32[32,2816]{1,0:T(8,128)}, u32[]{:S(2)}) copy-start(f32[32,2816]{1,0:T(8,128)} %get-tuple-element.136) | copy-start | bytes 1081348
  408.9 5.4 %copy-start.4 = (f32[88,1024]{1,0:T(8,128)S(1)}, f32[88,1024]{1,0:T(8,128)}, u32[]{:S(2)}) copy-start(f32[88,1024]{1,0:T(8,128)} %get-tuple-element.137) | copy-start | bytes 1081348
where the time goes:
time: 415 us
  Pallas kernels  337 us (81%)
  matrix products  56.8 us (14%)
  local copies, waits for them, and re-layouts  14.2 us (3%)
  other arithmetic  6.01 us (1%)
    pallas_call x1, Pallas kernels, forward(): pl.pallas_call(functools.partial(forward_kernel, planes, shapes, first_gr...  151 us
    pallas_call x1, Pallas kernels, scatter_sum(): pl.pallas_call(functools.partial(scatter_kernel, planes, shapes), out_sha...  140 us
    pallas_call x1, Pallas kernels, last(): pl.pallas_call(functools.partial(last_kernel, planes, shapes), out_shape=...  47 us
    dot_general x4, matrix products, on_device(): back = lambda a, b: lax.dot_general(a, b, NT, preferred_element_type=f32)  19.4 us
    dot_general x4, matrix products, on_device(): lax.dot_general(a, b, TN, preferred_element_type=f32).astype(bf16)  17.7 us
    unnamed x56, local copies, waits for them, and re-layouts  10.4 us

commit v1 on v0

--- a/solution.py
+++ b/solution.py
@@ -39,13 +39,10 @@
 
 
 def tables(segment_ids, rank, rows):
-    seqs, length = segment_ids.shape
-    places = jnp.arange(length, dtype=jnp.int32)
-    edges = jnp.concatenate(
-        [jnp.ones((seqs, 1), dtype=jnp.bool_), segment_ids[:, 1:] != segment_ids[:, :-1]], axis=1
-    )
-    starts = lax.cummax(jnp.where(edges, places[None, :], 0), axis=1)
-    starts = lax.dynamic_slice_in_dim(starts, rank * rows, rows, 1)
+    seqs = segment_ids.shape[0]
+    own_ids = lax.dynamic_slice_in_dim(segment_ids, rank * rows, rows, 1)
+    earlier = segment_ids[:, :, None] < own_ids[:, None, :]
+    starts = jnp.sum(earlier.astype(jnp.int32), axis=1)
     local = rank * rows + jnp.arange(rows, dtype=jnp.int32) - starts
     lane = jnp.arange(128, dtype=jnp.int32)
     half = HEAD_DIM // 2
@@ -380,7 +377,7 @@
             between()
             act(relay(g, zz, 1, False))
             return
-        lean = t > 0
+        lean = t < planes - 1
         pl.when(lean & (x == 1))(lambda: act(relay(g, zz, 1, True)))
         between()
         pl.when((x == 1) | jnp.logical_not(lean))(lambda: act(relay(g, zz, 1, False)))
@@ -908,6 +905,30 @@
                 send_b(s).start()
                 pl.when(x == 1)(lambda: send_d(s).start())
 
+    def finish(s):
+        send_b(s).wait_recv()
+        pl.when(x == 0)(lambda: send_back(s).wait_recv())
+
+        @pl.loop(0, rows // 32)
+        def _(i):
+            at = pl.ds(pl.multiple_of(i * 32, 32), 32)
+            flat = pl.ds(pl.multiple_of(s * rows + i * 32, 32), 32)
+            cos_rows, sin_rows = cos_table[flat, :], sin_table[flat, :]
+            for k in range(pairs):
+                lanes = pl.ds(k * 128, 128)
+
+                def summed(kind):
+                    return (
+                        mine[kind, s, at, lanes].astype(f32)
+                        + from_b[kind, s, at, lanes].astype(f32)
+                        + jnp.where(x == 0, chip[kind, s, at, lanes].astype(f32), 0.0)
+                    )
+
+                d_key[flat, lanes] = turned(summed(0), cos_rows, sin_rows, -1.0).astype(jnp.bfloat16)
+                half = 0.5 * summed(1)
+                d_value[flat, lanes] = half.astype(jnp.bfloat16)
+                first_grad[flat, lanes] = half
+
     @pl.loop(0, planes)
     def _(r):
         zz = visit(planes - 1 - r, z, planes)
@@ -927,48 +948,22 @@
         work(2 * r - 1)
         for g in range(n):
             pl.when(r >= 2)(lambda: steps.line(g, t + 2))
+        pl.when((r >= planes) & (r < planes + seqs))(lambda: finish(r - planes))
 
     @pl.loop(0, planes)
     def _(t):
         for g in range(n):
             steps.end(g, t)
 
+    for s in range(2, seqs):
+        finish(s)
     for s in range(seqs):
-        send_b(s).wait()
-
-        @pl.when(x == 0)
-        def _():
-            send_back(s).wait_recv()
+        send_b(s).wait_send()
 
         @pl.when(x == 1)
         def _():
             send_d(s).wait_send()
             send_back(s).wait_send()
-
-    @pl.when(x == 1)
-    def _():
-        chip[...] = jnp.zeros_like(chip)
-
-    @pl.loop(0, seqs * rows // 32)
-    def _(i):
-        seq = lax.div(i, rows // 32)
-        at = pl.ds(pl.multiple_of(lax.rem(i, rows // 32) * 32, 32), 32)
-        flat = pl.ds(pl.multiple_of(i * 32, 32), 32)
-        cos_rows, sin_rows = cos_table[flat, :], sin_table[flat, :]
-        for k in range(pairs):
-            lanes = pl.ds(k * 128, 128)
-
-            def summed(kind):
-                return (
-                    mine[kind, seq, at, lanes].astype(f32)
-                    + from_b[kind, seq, at, lanes].astype(f32)
-                    + chip[kind, seq, at, lanes].astype(f32)
-                )
-
-            d_key[flat, lanes] = turned(summed(0), cos_rows, sin_rows, -1.0).astype(jnp.bfloat16)
-            half = 0.5 * summed(1)
-            d_value[flat, lanes] = half.astype(jnp.bfloat16)
-            first_grad[flat, lanes] = half
 
 
 def boxes_of(planes, shapes, types):
@@ -1083,11 +1078,15 @@
             shape = (at_once, 2, 2, 2, *shapes[g])
             parts[g][pl.ds(j * at_once, at_once)] = part.reshape(shape).astype(bf16)
 
-    def normed_grad():
-        for copy in loads:
-            copy.wait()
-
-        @pl.loop(0, width // 256)
+    each = max(width // 256 // planes, 1)
+
+    def normed_grad(r):
+        @pl.when(r == 0)
+        def _():
+            for copy in loads:
+                copy.wait()
+
+        @pl.loop(r * each, r * each + each)
         def _(j):
             at = pl.ds(pl.multiple_of(j * 256, 256), 256)
             total = 0.0
@@ -1128,9 +1127,7 @@
 
     if at_once > 1:
         pl.loop(0, width // 256)(weight_grads)
-    lag = 2
-
-    @pl.loop(0, planes + 3 + lag)
+    @pl.loop(0, planes + 4)
     def _(r):
         t = planes - 1 - r
 
@@ -1141,17 +1138,21 @@
             for g in range(3):
                 send_cores(g, t)
 
-        for group, late in ((range(3), 0), ((3,), lag)):
-            for step, behind in ((steps.core, 1), (steps.plane, 2), (steps.line, 3)):
-                behind += late
-                for g in group:
-                    pl.when((r >= behind) & (r < planes + behind))(lambda: step(g, t + behind))
-
-        @pl.when(r == 1)
+        for behind, step in ((1, steps.core), (2, steps.plane), (3, steps.line)):
+            for g in range(3):
+                pl.when((r >= behind) & (r < planes + behind))(lambda: step(g, t + behind))
+
+            @pl.when(r == planes + behind)
+            def _():
+                @pl.loop(0, planes)
+                def _(i):
+                    step(3, planes - 1 - i)
+
+        @pl.when(r < width // 256 // each)
         def _():
-            normed_grad()
-
-        @pl.when(r == 2)
+            normed_grad(r)
+
+        @pl.when(r == planes)
         def _():
             token_gradient()
 
@@ -1194,6 +1195,24 @@
     )(normed, *d_proj, *weights, tok, d_residual, attn_gain, d_ffn_gain)
 
 
+def deliver(arrays):
+    n = len(arrays)
+
+    def kernel(*refs):
+        for src, dst in zip(refs[:n], refs[n:]):
+            dst[...] = src[...]
+
+    specs = [pl.BlockSpec((a.shape[0], a.shape[1] // 2), lambda i: (0, i)) for a in arrays]
+    return pl.pallas_call(
+        kernel,
+        grid=(2,),
+        in_specs=specs,
+        out_specs=specs,
+        out_shape=[jax.ShapeDtypeStruct(a.shape, a.dtype) for a in arrays],
+        name="deliver",
+    )(*arrays)
+
+
 def on_device(
     planes,
     tokens,
@@ -1217,9 +1236,12 @@
     per = 128 // share
     index = lax.axis_index("dp") * lax.axis_size("ctx") + rank
     place = lax.rem(index, per)
-    here = jnp.arange(128, dtype=jnp.int32) // share == place
-    spread = lambda gain: jnp.where(here, jnp.tile(gain, per), jnp.zeros((), bf16))
-    gains = jnp.zeros((16, 128), bf16).at[0].set(spread(attn_gain)).at[1].set(spread(ffn_gain))
+    lane = jnp.arange(128, dtype=jnp.int32)[None, :] - place * share
+    here = lane == jnp.arange(share, dtype=jnp.int32)[:, None]
+    spread = lambda gain: jnp.sum(jnp.where(here, gain.astype(f32)[:, None], 0.0), axis=0)
+    kind = jnp.arange(16, dtype=jnp.int32)[:, None]
+    gains = jnp.where(kind == 0, spread(attn_gain), jnp.where(kind == 1, spread(ffn_gain), 0.0))
+    gains = gains.astype(bf16)
     starts, cos_table, sin_table = tables(segment_ids, rank, rows)
     flat = (seqs * rows, width)
     local = (seqs, rows, width)
@@ -1293,6 +1315,9 @@
         d_residual,
         attn_gain.astype(f32),
         d_ffn_gain[None],
+    )
+    token_grad, first_grad, s_wq, s_wk, s_wv, s_out, s_gate, s_up, s_down = deliver(
+        [token_grad, first_grad, s_wq, s_wk, s_wv, s_out, s_gate, s_up, s_down]
     )
     slot = lax.rem(index, 256 // share) * share
     s_gains = lax.dynamic_slice_in_dim(s_gains[:2], slot, share, 1)

time: 415 us -> 400 us (0.964)
  local copies, waits for them, and re-layouts: 14.2 us -> 3.59 us
  Pallas kernels: 337 us -> 331 us
    unnamed x56 -> x27, local copies, waits for them, and re-layouts: 10.4 us -> 1.03 us
    pallas_call x1, Pallas kernels: 140 us -> 132 us  [scatter_sum(): pl.pallas_call(functools.partial(scatter_kernel, planes, shapes), out_sha...]
    pallas_call x1, Pallas kernels: 151 us -> 145 us  [forward(): pl.pallas_call(functools.partial(forward_kernel, planes, shapes, first_gr...]
    pallas_call x0 -> x1, Pallas kernels: none -> 4.44 us  [deliver(): pl.pallas_call(kernel, grid=(2,), in_specs=specs, out_specs=specs, out_sh...]
where the time goes in v1:
time: 400 us
  Pallas kernels  331 us (83%)
  matrix products  57 us (14%)
  other arithmetic  7.33 us (2%)
    pallas_call x1, Pallas kernels, forward(): pl.pallas_call(functools.partial(forward_kernel, planes, shapes, first_gr...  145 us
    pallas_call x1, Pallas kernels, scatter_sum(): pl.pallas_call(functools.partial(scatter_kernel, planes, shapes), out_sha...  132 us
    pallas_call x1, Pallas kernels, last(): pl.pallas_call(functools.partial(last_kernel, planes, shapes), out_shape=...  49.8 us
    dot_general x4, matrix products, on_device(): back = lambda a, b: lax.dot_general(a, b, NT, preferred_element_type=f32)  19.4 us
    dot_general x4, matrix products, on_device(): lax.dot_general(a, b, TN, preferred_element_type=f32).astype(bf16)  17.8 us

profile of v1, /device:TPU:0, one launch (start us, length us, event | category | flops | bytes accessed | tf_op | source)
XLA Modules:
  0.0 399.6 jit_solution(15212705895843979669)
XLA Ops:
  0.7 0.7 convert_element_type.95
  2.1 0.7 constant_dynamic-slice_fusion.1
  2.8 1.0 convert_reduce_fusion
  4.4 0.7 select_convert_fusion.refs_0_
  5.1 1.8 fusion.7
  6.9 144.7 %forward.1 = (bf16[1,4,2,2,2,16,128]{6,5,4,3,2,1,0:T(8,128)(2,1)}, bf16[1,4,2,2,2,32,1024]{6,5,4,3,2,1,0:T(8,128)(2,1)}, bf16[1,4,2,2,2,32,1024]{6,5,4,3,2,1,0:T...) custom-call(bf16[1,16,128]{2,1,0:T(8,128)(2,1)} %select_convert_fusi, ...), custom_call_target="tpu_custom_call" | custom-call | tf_op jit(solution)/shard_map/forward/pallas_call | solution.py:538
  151.6 0.9 reduce_sum.72
  153.2 3.7 multiply_reduce_fusion.2
  157.2 4.9 %fusion.14 = f32[512,2816]{1,0:T(8,128)} fusion(bf16[512,1024]{1,0:T(8,128)(2,1)S(1)} %multiply_convert_fusion.1, bf16[1024,2816]{1,0:T(8,128)(2,1)S(1)} %bitcast.105), kind=kOutput, calls=%fused_computation.55 | convolution fusion | flops 2952790016 | bytes 12582912 | tf_op jit(solution)/shard_map/dot_general | solution.py:1278
  162.1 5.0 %fusion.13 = f32[512,2816]{1,0:T(8,128)} fusion(bf16[512,1024]{1,0:T(8,128)(2,1)S(1)} %multiply_convert_fusion.1, bf16[1024,2816]{1,0:T(8,128)(2,1)S(1)} %bitcast.109), kind=kOutput, calls=%fused_computation.54 | convolution fusion | flops 2952790016 | bytes 12582912 | tf_op jit(solution)/shard_map/dot_general | solution.py:1277
  167.2 9.9 %fusion.3 = (bf16[512,2816]{1,0:T(8,128)(2,1)S(1)}, bf16[512,2816]{1,0:T(8,128)(2,1)}, bf16[512,2816]{1,0:T(8,128)(2,1)}) fusion(f32[512,2816]{1,0:T(8,128)} %fusion.13, f32[512,2816]{1,0:T(8,128)} %fusion.14, bf16[2816,1024]{1,0:T(8,128)(2,1)S(1)} %bitcast.113, bf16[512,1024]{1,0:T(8,128)(2,1)S(1)} %bitcast.82), kind=kOutput, calls=%fused_computation.5 | convolution fusion | flops 2974416896 | bytes 27000832 | tf_op jit(solution)/shard_map/dot_general | solution.py:1251
  177.1 6.1 %add_convert_fusion = bf16[512,1024]{1,0:T(8,128)(2,1)} fusion(f32[512,1024]{1,0:T(8,128)S(1)} %get-tuple-element.104, bf16[512,2816]{1,0:T(8,128)(2,1)} %get-tuple-element.94, bf16[2816,1024]{1,0:T(8,128)(2,1)S(1)} %bitcast.114), kind=kOutput, calls=%fused_computation.15 | convolution fusion | flops 2953838592 | bytes 11796480 | tf_op jit(solution)/shard_map/dot_general | solution.py:1280
  183.2 3.2 fusion.15
  186.4 4.1 %multiply_reduce_fusion = (f32[1024]{0:T(1024)}, f32[512]{0:T(512)S(1)}, f32[512,1024]{1,0:T(8,128)S(1)}) fusion(f32[512,1024]{1,0:T(8,128)S(1)} %get-tuple-element.104, f32[512]{0:T(512)S(1)} %get-tuple-element.100, f32[1024]{0:T(1024)S(1)} %bitcast.98, f32[512,1024]{1,0:T(8,128)S(1)} %fusion.15, bf16[512,2816]{1,0:T(8,128)(2,1)S(1)} %get-tuple-element.92, ...), kind=kOutput, calls=%fused_computation.12 | convolution fusion | flops 2956458496 | bytes 14954496 | tf_op jit(solution)/shard_map/dot_general | solution.py:1251
  191.1 1.0 copy-done.3
  192.0 2.3 convolution_convert_fusion.4
  194.4 2.6 convolution_convert_fusion.3
  197.0 5.1 %convolution_convert_fusion = bf16[1024,2816]{1,0:T(8,128)(2,1)} fusion(bf16[512,1024]{1,0:T(8,128)(2,1)S(1)} %multiply_convert_fusion.1, bf16[512,2816]{1,0:T(8,128)(2,1)S(1)} %get-tuple-element.92), kind=kOutput, calls=%fused_computation.9 | convolution fusion | flops 2955673600 | bytes 9699328 | tf_op jit(solution)/shard_map/dot_general | solution.py:1250
  202.1 5.1 %convolution_convert_fusion.1 = bf16[1024,2816]{1,0:T(8,128)(2,1)} fusion(bf16[512,1024]{1,0:T(8,128)(2,1)S(1)} %multiply_convert_fusion.1, bf16[512,2816]{1,0:T(8,128)(2,1)S(1)} %copy-done.6), kind=kOutput, calls=%fused_computation.10 | convolution fusion | flops 2955673600 | bytes 9699328 | tf_op jit(solution)/shard_map/dot_general | solution.py:1250
  207.2 5.0 %convolution_convert_fusion.2 = bf16[2816,1024]{1,0:T(8,128)(2,1)} fusion(bf16[512,2816]{1,0:T(8,128)(2,1)S(1)} %copy-done.4, bf16[512,1024]{1,0:T(8,128)(2,1)S(1)} %bitcast.83), kind=kOutput, calls=%fused_computation.11 | convolution fusion | flops 2955673600 | bytes 9699328 | tf_op jit(solution)/shard_map/dot_general | solution.py:1250
  212.2 132.0 %gradient_scatter.1 = (f32[88,1024]{1,0:T(8,128)}, f32[32,2816]{1,0:T(8,128)}, f32[32,2816]{1,0:T(8,128)}, f32[32,1024]{1,0:T(8,128)}, bf16[2,256,1024]{2,1,0:T(...) custom-call(bf16[4,2,2,2,88,1024]{5,4,3,2,1,0:T(8,128)(2,1)} %bitcast.74, ...), custom_call_target="tpu_custom_call" | custom-call | tf_op jit(solution)/shard_map/gradient_scatter/pallas_call | solution.py:1015
  344.1 49.8 %last.1 = (f32[32,1024]{1,0:T(8,128)}, f32[32,1024]{1,0:T(8,128)}, f32[32,1024]{1,0:T(8,128)}, f32[8,256]{1,0:T(8,128)}, f32[512,1024]{1,0:T(8,128)}) custom-call(bf16[512,1024]{1,0:T(8,128)(2,1)} %get-tuple-element.56.refs_0_, bf16[512,1024]{1,0:T(8,128)(2,1)} %bitcast.86, bf16[512,1024]{1,0:T(8,128)(2,1)} %get-tuple-element.64.refs_2_, ...), custom_call_target="tpu_custom_call" | custom-call | tf_op jit(solution)/shard_map/last/pallas_call | solution.py:1176
  393.9 4.4 %deliver.1 = (f32[512,1024]{1,0:T(8,128)}, f32[512,1024]{1,0:T(8,128)}, f32[32,1024]{1,0:T(8,128)}, f32[32,1024]{1,0:T(8,128)}, f32[32,1024]{1,0:T(8,128)}, /*in...) custom-call(f32[512,1024]{1,0:T(8,128)} %get-tuple-element.69.refs_0_, ...), custom_call_target="tpu_custom_call" | custom-call | tf_op jit(solution)/shard_map/deliver/pallas_call | solution.py:1206
  398.3 0.7 slice.17
  (45 shorter events, 3.5 us)
Async XLA Ops:
  153.2 3.9 slice-start
  153.2 4.0 slice-start.1
  156.9 5.2 %slice-start.2 = ((s8[5767168]{0:T(1024)(128)(4,1)}), s8[4194304]{0:T(1024)(128)(4,1)S(1)}, s32[]{:S(2)}) async-start(s8[5767168]{0:T(1024)(128)(4,1)} %bitcast.107), calls=%async_computation.2 | async-start | bytes 8388608
  157.2 5.0 %slice-start.3 = ((s8[5767168]{0:T(1024)(128)(4,1)}), s8[1572864]{0:T(1024)(128)(4,1)S(1)}, s32[]{:S(2)}) async-start(s8[5767168]{0:T(1024)(128)(4,1)} %bitcast.107), calls=%async_computation.3 | async-start | bytes 3145728
  157.2 10.0 %slice-start.4 = ((s8[5767168]{0:T(1024)(128)(4,1)}), s8[4194304]{0:T(1024)(128)(4,1)S(1)}, s32[]{:S(2)}) async-start(s8[5767168]{0:T(1024)(128)(4,1)} %bitcast.111), calls=%async_computation.4 | async-start | bytes 8388608
  162.1 5.0 %copy-start.1 = (bf16[2,256,1024]{2,1,0:T(8,128)(2,1)S(1)}, bf16[2,256,1024]{2,1,0:T(8,128)(2,1)}, u32[]{:S(2)}) copy-start(bf16[2,256,1024]{2,1,0:T(8,128)(2,1)} %param.15) | copy-start | bytes 3145732
  162.1 5.0 %slice-start.5 = ((s8[5767168]{0:T(1024)(128)(4,1)}), s8[1572864]{0:T(1024)(128)(4,1)S(1)}, s32[]{:S(2)}) async-start(s8[5767168]{0:T(1024)(128)(4,1)} %bitcast.111), calls=%async_computation.5 | async-start | bytes 3145728
  177.1 6.2 %copy-start.5 = (bf16[512,2816]{1,0:T(8,128)(2,1)S(1)}, bf16[512,2816]{1,0:T(8,128)(2,1)}, u32[]{:S(2)}) copy-start(bf16[512,2816]{1,0:T(8,128)(2,1)} %get-tuple-element.93) | copy-start | bytes 8650756
  190.4 1.6 copy-start.3
  192.0 2.4 copy-start
  192.0 2.4 copy-start.2
  197.0 5.1 %copy-start.6 = (bf16[512,2816]{1,0:T(8,128)(2,1)S(1)}, bf16[512,2816]{1,0:T(8,128)(2,1)}, u32[]{:S(2)}) copy-start(bf16[512,2816]{1,0:T(8,128)(2,1)} %get-tuple-element.93) | copy-start | bytes 8650756
  202.1 5.1 %copy-start.4 = (bf16[512,2816]{1,0:T(8,128)(2,1)S(1)}, bf16[512,2816]{1,0:T(8,128)(2,1)}, u32[]{:S(2)}) copy-start(bf16[512,2816]{1,0:T(8,128)(2,1)} %get-tuple-element.94) | copy-start | bytes 8650756

commit v2 on v1

--- a/solution.py
+++ b/solution.py
@@ -281,8 +281,14 @@
     ins, refs = refs[:n], refs[n:]
     tok, first, starts, cos_table, sin_table = refs[:5]
     outs, refs = refs[5 : 5 + n], refs[5 + n :]
-    normed, query, mine, near, chip, far, context, log_total = refs[:8]
-    sems, refs = refs[8:19], refs[19:]
+    *results, log_total, attn_gain, ffn_gain = refs[:10]
+    sems, refs = refs[10:21], refs[21:]
+    normed, query, mine, near, chip, far, context = held = refs[:7]
+    store_sem, refs = refs[7], refs[8:]
+    stores = [
+        pltpu.make_async_copy(src, dst, store_sem.at[i])
+        for i, (src, dst) in enumerate(zip(held, results))
+    ]
     own_sem, z_send, z_recv, x_send, x_recv, y_send, y_recv, d_send, d_recv, c_send, c_recv = sems
     tile_send, tile_recv, load_sem, gains, *weights = refs[: 4 + first_group - 1]
     scratch = refs[4 + first_group - 1 :]
@@ -451,12 +457,14 @@
         per = len(flat_gains) * 128 // width
         gain = jnp.concatenate(
             [
-                sum(b[:1].astype(jnp.float32) for b in flat_gains[i * per : (i + 1) * per])
+                sum(b[:2].astype(jnp.float32) for b in flat_gains[i * per : (i + 1) * per])
                 for i in range(width // 128)
             ],
             axis=1,
         )
-        normalise(tok, gain, normed)
+        attn_gain[...] = gain[:1]
+        ffn_gain[...] = gain[1:]
+        normalise(tok, gain[:1], normed)
         for copy in loads[1:]:
             copy.wait()
         as_blocks = lambda w: w.reshape((planes * 8, *w.shape[4:]))
@@ -465,6 +473,8 @@
         )
         for s in range(seqs):
             send_tiles(s)
+        for copy in stores[:3]:
+            copy.start()
 
     def unit(s, p):
         lanes = pl.ds(pl.multiple_of(p * 128, 128), 128)
@@ -494,6 +504,14 @@
             def _(p):
                 unit(s, p)
 
+        for copy in (stores[3], stores[6]):
+            copy.start()
+
+        @pl.when(x == 1)
+        def _():
+            stores[4].start()
+            stores[5].start()
+
     groups = (range(first_group), range(first_group, n))
 
     @pl.loop(0, 2 * planes + 2)
@@ -521,6 +539,13 @@
         to_partner(s).wait_send()
         pl.when(x == 0)(lambda: to_x(s).wait_send())
         pl.when(x == 1)(lambda: passed_on(s).wait_send())
+    for copy in (*stores[:4], stores[6]):
+        copy.wait()
+
+    @pl.when(x == 1)
+    def _():
+        stores[4].wait()
+        stores[5].wait()
 
 
 def forward(planes, first_group, blocks, tok, first, starts, cos_table, sin_table):
@@ -542,9 +567,10 @@
             for s, b in zip(shapes, blocks)
         ]
         + [jax.ShapeDtypeStruct(tok.shape, bf16), local, *[tile] * 4, local]
-        + [jax.ShapeDtypeStruct((seqs, width // 128, 1, 2 * rows), jnp.float32)],
+        + [jax.ShapeDtypeStruct((seqs, width // 128, 1, 2 * rows), jnp.float32)]
+        + [jax.ShapeDtypeStruct((1, width), jnp.float32)] * 2,
         in_specs=[anywhere] * n + [vmem] * 5,
-        out_specs=[anywhere] * n + [vmem] * 8,
+        out_specs=[anywhere] * (n + 7) + [vmem] * 3,
         scratch_shapes=[
             dma((n,)),
             dma((n, planes, 2)),
@@ -557,6 +583,8 @@
             dma((n, planes, 2)),
             dma((n, planes)),
             dma((n, planes)),
+            *[pltpu.VMEM(h.shape, bf16) for h in [tok, local, *[tile] * 4, local]],
+            dma((7,)),
             dma((3, seqs)),
             dma((3, seqs)),
             dma((first_group,)),
@@ -677,7 +705,7 @@
         if not routed:
             even()
             return
-        is_lean = (x == 1) & (t < planes - 2)
+        is_lean = (x == 1) & (t < planes - 1)
         pl.when(jnp.logical_not(is_lean))(even)
         pl.when(is_lean)(lean)
 
@@ -695,7 +723,7 @@
         add(own_at(g, zz, 1 - y, x), from_core[g].at[zz, 1 - y, x])
         if routed:
 
-            @pl.when((x == 0) & (t < planes - 2))
+            @pl.when((x == 0) & (t < planes - 1))
             def _():
                 y_copy(g, zz).start()
 
@@ -720,7 +748,7 @@
             take_x()
             take_y(False)
             return
-        lean = t < planes - 2
+        lean = t < planes - 1
         pl.when((x == 1) | jnp.logical_not(lean))(take_x)
         pl.when((x == 1) & lean)(lambda: take_y(True))
         pl.when((x == 0) | jnp.logical_not(lean))(lambda: take_y(False))
@@ -802,9 +830,11 @@
 def scatter_kernel(planes, shapes, *refs):
     n = len(shapes)
     parts, refs = refs[:n], refs[n:]
-    starts, query, *tiles, context, d_context, log_total, cos_table, sin_table = refs[:11]
+    starts, log_total, cos_table, sin_table, *sources = refs[:11]
     refs = refs[11:]
     outs, refs = refs[:n], refs[n:]
+    query, *tiles, context, d_context = held = refs[-8:-1]
+    source_sem, refs = refs[-1], refs[:-8]
     d_query, d_key, d_value, first_grad = refs[:4]
     refs = refs[4:]
     mine, near, chip, far, from_b, from_d, tile_send, tile_recv, bias, acc = refs[-10:]
@@ -892,6 +922,11 @@
 
             send_back(s).start()
 
+        @pl.when(i == 0)
+        def _():
+            for copy in sources:
+                copy.wait()
+
         @pl.when((i >= 0) & (i < 2 * seqs))
         def _():
             s = lax.div(i, 2)
@@ -935,6 +970,13 @@
         for g in range(n):
             steps.core_copy(g, zz).start()
             load(g, zz).start()
+
+    sources = [
+        pltpu.make_async_copy(src, dst, source_sem.at[i])
+        for i, (src, dst) in enumerate(zip(sources, held))
+    ]
+    for copy in sources:
+        copy.start()
 
     @pl.loop(0, planes + 2)
     def _(r):
@@ -1008,10 +1050,11 @@
     shapes = [p.shape[4:] for p in partials]
     bf16 = jnp.bfloat16
     dma = pltpu.SemaphoreType.DMA
-    box = attention[2].shape
+    attention, held = attention[:4], attention[4:]
+    box = held[1].shape
     seqs, rows, width = box[1:]
     flat = (seqs * rows, width)
-    vmem = pl.BlockSpec(memory_space=pltpu.VMEM)
+    vmem, anywhere = pl.BlockSpec(memory_space=pltpu.VMEM), pl.BlockSpec(memory_space=pl.ANY)
     return pl.pallas_call(
         functools.partial(scatter_kernel, planes, shapes),
         out_shape=[jax.ShapeDtypeStruct(s, jnp.float32) for s in shapes]
@@ -1021,7 +1064,7 @@
             jax.ShapeDtypeStruct(flat, bf16),
             jax.ShapeDtypeStruct(flat, jnp.float32),
         ],
-        in_specs=[pl.BlockSpec(memory_space=pl.ANY)] * n + [vmem] * len(attention),
+        in_specs=[anywhere] * n + [vmem] * len(attention) + [anywhere] * len(held),
         out_specs=[vmem] * (n + 4),
         scratch_shapes=[
             *[pltpu.VMEM((planes, 2, 2, *s), bf16) for s in shapes],
@@ -1032,12 +1075,14 @@
             dma((3, seqs)),
             dma((3, seqs)),
             *attend_back_scratch(rows),
+            *[pltpu.VMEM(h.shape, h.dtype) for h in held],
+            dma((len(held),)),
         ],
         compiler_params=pltpu.CompilerParams(
             collective_id=1, has_side_effects=True, vmem_limit_bytes=67043328
         ),
         name="gradient_scatter",
-    )(*partials, *attention)
+    )(*partials, *attention, *held)
 
 
 def last_kernel(planes, shapes, *refs):
@@ -1073,8 +1118,9 @@
 
     def weight_grads(j):
         lanes = pl.ds(pl.multiple_of(j * 256, 256), 256)
+        block = normed[:, lanes].T
         for g in range(3):
-            part = lax.dot_general(normed[:, lanes], d_proj[g][...], TN, preferred_element_type=f32)
+            part = jnp.dot(block, d_proj[g][...], preferred_element_type=f32)
             shape = (at_once, 2, 2, 2, *shapes[g])
             parts[g][pl.ds(j * at_once, at_once)] = part.reshape(shape).astype(bf16)
 
@@ -1249,12 +1295,14 @@
     mm = functools.partial(jnp.dot, preferred_element_type=f32)
     by_rows = lambda a, b: lax.dot_general(a, b, TN, preferred_element_type=f32).astype(bf16)
     back = lambda a, b: lax.dot_general(a, b, NT, preferred_element_type=f32)
-    (gains, w_query, w_key, w_value, w_out, gate_weight, up_weight, down_weight), (
+    (_, w_query, w_key, w_value, w_out, gate_weight, up_weight, down_weight), (
         normed_one,
         query_rot,
         *tiles,
         context3,
         log_total,
+        attn_gain,
+        ffn_gain,
     ) = forward(
         planes,
         4,
@@ -1265,15 +1313,12 @@
         cos_table,
         sin_table,
     )
-    gains = jnp.sum(gains.reshape(width // 128, per, 16, 128), axis=1)
-    attn_gain = gains[:, 0].reshape(1, width)
-    ffn_gain = gains[:, 1].reshape(1, width)
     context = context3.reshape(flat)
     tokens_float = tokens.astype(f32)
     cotangent = cotangent.reshape(flat)
     residual = tokens_float + mm(context, w_out)
     scale_two = inverse_rms(residual)
-    second_normed = (residual * scale_two * ffn_gain.astype(f32)).astype(bf16)
+    second_normed = (residual * scale_two * ffn_gain).astype(bf16)
     gate = mm(second_normed, gate_weight)
     up = mm(second_normed, up_weight)
     hidden = (swish(gate) * up).astype(bf16)
@@ -1289,7 +1334,7 @@
     d_up_weight = by_rows(second_normed, d_up)
     d_normed_two = back(d_gate, gate_weight) + back(d_up, up_weight)
     d_ffn_gain = jnp.sum(d_normed_two * residual * scale_two, axis=0)
-    weighted_two = d_normed_two * ffn_gain.astype(f32)
+    weighted_two = d_normed_two * ffn_gain
     d_residual = (
         out_float
         + scale_two * weighted_two
@@ -1303,7 +1348,7 @@
     s_down, s_gate, s_up, s_out, d_query, d_key, d_value, first_grad = scatter_sum(
         planes,
         [d_down, d_gate_weight, d_up_weight, d_out],
-        [starts, query_rot, *tiles, context3, d_context, log_total, cos_table, sin_table],
+        [starts, log_total, cos_table, sin_table, query_rot, *tiles, context3, d_context],
     )
     d_query = d_query.reshape(flat)
     s_wq, s_wk, s_wv, s_gains, token_grad = last(
@@ -1313,7 +1358,7 @@
         [w_query, w_key, w_value],
         tokens,
         d_residual,
-        attn_gain.astype(f32),
+        attn_gain,
         d_ffn_gain[None],
     )
     token_grad, first_grad, s_wq, s_wk, s_wv, s_out, s_gate, s_up, s_down = deliver(

time: 400 us -> 391 us (0.978)
  Pallas kernels: 331 us -> 324 us
where the time goes in v2:
time: 391 us
  Pallas kernels  324 us (83%)
  matrix products  56.9 us (15%)
  other arithmetic  5.8 us (1%)
    pallas_call x1, Pallas kernels, forward(): pl.pallas_call(functools.partial(forward_kernel, planes, shapes, first_gr...  141 us
    pallas_call x1, Pallas kernels, scatter_sum(): pl.pallas_call(functools.partial(scatter_kernel, planes, shapes), out_sha...  128 us
    pallas_call x1, Pallas kernels, last(): pl.pallas_call(functools.partial(last_kernel, planes, shapes), out_shape=...  49.8 us
    dot_general x4, matrix products, on_device(): back = lambda a, b: lax.dot_general(a, b, NT, preferred_element_type=f32)  19.5 us
    dot_general x4, matrix products, on_device(): lax.dot_general(a, b, TN, preferred_element_type=f32).astype(bf16)  17.7 us

profile of v2, /device:TPU:0, one launch (start us, length us, event | category | flops | bytes accessed | tf_op | source)
XLA Modules:
  0.0 391.0 jit_solution(10335745987443717245)
XLA Ops:
  0.7 0.7 convert_element_type.76
  1.3 0.7 convert_element_type.77
  2.1 0.7 constant_dynamic-slice_fusion.1
  2.8 1.0 convert_reduce_fusion
  4.4 0.7 select_convert_fusion.refs_0_
  5.1 1.8 fusion.7
  6.9 141.2 %forward.1 = (bf16[1,4,2,2,2,16,128]{6,5,4,3,2,1,0:T(8,128)(2,1)}, bf16[1,4,2,2,2,32,1024]{6,5,4,3,2,1,0:T(8,128)(2,1)}, bf16[1,4,2,2,2,32,1024]{6,5,4,3,2,1,0:T...) custom-call(bf16[1,16,128]{2,1,0:T(8,128)(2,1)} %select_convert_fusi, ...), custom_call_target="tpu_custom_call" | custom-call | tf_op jit(solution)/shard_map/forward/pallas_call | solution.py:563
  148.2 3.7 multiply_reduce_fusion.2
  152.2 4.9 %fusion.13 = f32[512,2816]{1,0:T(8,128)} fusion(bf16[512,1024]{1,0:T(8,128)(2,1)S(1)} %multiply_convert_fusion.1, bf16[1024,2816]{1,0:T(8,128)(2,1)S(1)} %bitcast.101), kind=kOutput, calls=%fused_computation.52 | convolution fusion | flops 2952790016 | bytes 12582912 | tf_op jit(solution)/shard_map/dot_general | solution.py:1323
  157.1 5.0 %fusion.12 = f32[512,2816]{1,0:T(8,128)} fusion(bf16[512,1024]{1,0:T(8,128)(2,1)S(1)} %multiply_convert_fusion.1, bf16[1024,2816]{1,0:T(8,128)(2,1)S(1)} %bitcast.105), kind=kOutput, calls=%fused_computation.51 | convolution fusion | flops 2952790016 | bytes 12582912 | tf_op jit(solution)/shard_map/dot_general | solution.py:1322
  162.1 9.9 %fusion.3 = (bf16[512,2816]{1,0:T(8,128)(2,1)S(1)}, bf16[512,2816]{1,0:T(8,128)(2,1)}, bf16[512,2816]{1,0:T(8,128)(2,1)}) fusion(f32[512,2816]{1,0:T(8,128)} %fusion.12, f32[512,2816]{1,0:T(8,128)} %fusion.13, bf16[2816,1024]{1,0:T(8,128)(2,1)S(1)} %bitcast.109, bf16[512,1024]{1,0:T(8,128)(2,1)S(1)} %bitcast.80), kind=kOutput, calls=%fused_computation.5 | convolution fusion | flops 2974416896 | bytes 27000832 | tf_op jit(solution)/shard_map/dot_general | solution.py:1297
  172.1 6.1 %add_convert_fusion = bf16[512,1024]{1,0:T(8,128)(2,1)} fusion(f32[512,1024]{1,0:T(8,128)S(1)} %get-tuple-element.104, bf16[512,2816]{1,0:T(8,128)(2,1)} %get-tuple-element.96, bf16[2816,1024]{1,0:T(8,128)(2,1)S(1)} %bitcast.110), kind=kOutput, calls=%fused_computation.15 | convolution fusion | flops 2953838592 | bytes 11796480 | tf_op jit(solution)/shard_map/dot_general | solution.py:1325
  178.2 3.2 fusion.14
  181.4 4.0 %multiply_reduce_fusion = (f32[1024]{0:T(1024)}, f32[512]{0:T(512)S(1)}, f32[512,1024]{1,0:T(8,128)S(1)}) fusion(f32[512,1024]{1,0:T(8,128)S(1)} %get-tuple-element.104, f32[512]{0:T(512)S(1)} %get-tuple-element.100, f32[1024]{0:T(1024)S(1)} %bitcast.95, f32[512,1024]{1,0:T(8,128)S(1)} %fusion.14, bf16[512,2816]{1,0:T(8,128)(2,1)S(1)} %get-tuple-element.94, ...), kind=kOutput, calls=%fused_computation.12 | convolution fusion | flops 2956458496 | bytes 14954496 | tf_op jit(solution)/shard_map/dot_general | solution.py:1297
  186.0 1.0 copy-done.4
  187.0 2.3 convolution_convert_fusion.4
  189.3 2.6 convolution_convert_fusion.3
  192.0 5.1 %convolution_convert_fusion = bf16[1024,2816]{1,0:T(8,128)(2,1)} fusion(bf16[512,1024]{1,0:T(8,128)(2,1)S(1)} %multiply_convert_fusion.1, bf16[512,2816]{1,0:T(8,128)(2,1)S(1)} %get-tuple-element.94), kind=kOutput, calls=%fused_computation.9 | convolution fusion | flops 2955673600 | bytes 9699328 | tf_op jit(solution)/shard_map/dot_general | solution.py:1296
  197.0 5.1 %convolution_convert_fusion.1 = bf16[1024,2816]{1,0:T(8,128)(2,1)} fusion(bf16[512,1024]{1,0:T(8,128)(2,1)S(1)} %multiply_convert_fusion.1, bf16[512,2816]{1,0:T(8,128)(2,1)S(1)} %copy-done.7), kind=kOutput, calls=%fused_computation.10 | convolution fusion | flops 2955673600 | bytes 9699328 | tf_op jit(solution)/shard_map/dot_general | solution.py:1296
  202.1 5.0 %convolution_convert_fusion.2 = bf16[2816,1024]{1,0:T(8,128)(2,1)} fusion(bf16[512,2816]{1,0:T(8,128)(2,1)S(1)} %copy-done.5, bf16[512,1024]{1,0:T(8,128)(2,1)S(1)} %bitcast.81), kind=kOutput, calls=%fused_computation.11 | convolution fusion | flops 2955673600 | bytes 9699328 | tf_op jit(solution)/shard_map/dot_general | solution.py:1296
  207.1 128.4 %gradient_scatter.1 = (f32[88,1024]{1,0:T(8,128)}, f32[32,2816]{1,0:T(8,128)}, f32[32,2816]{1,0:T(8,128)}, f32[32,1024]{1,0:T(8,128)}, bf16[2,256,1024]{2,1,0:T(...) custom-call(bf16[4,2,2,2,88,1024]{5,4,3,2,1,0:T(8,128)(2,1)} %bitcast.72, ...), custom_call_target="tpu_custom_call" | custom-call | tf_op jit(solution)/shard_map/gradient_scatter/pallas_call | solution.py:1058
  335.5 49.8 %last.1 = (f32[32,1024]{1,0:T(8,128)}, f32[32,1024]{1,0:T(8,128)}, f32[32,1024]{1,0:T(8,128)}, f32[8,256]{1,0:T(8,128)}, f32[512,1024]{1,0:T(8,128)}) custom-call(bf16[512,1024]{1,0:T(8,128)(2,1)} %get-tuple-element.57.refs_0_, bf16[512,1024]{1,0:T(8,128)(2,1)} %bitcast.84, bf16[512,1024]{1,0:T(8,128)(2,1)} %get-tuple-element.65.refs_2_, ...), custom_call_target="tpu_custom_call" | custom-call | tf_op jit(solution)/shard_map/last/pallas_call | solution.py:1222
  385.3 4.4 %deliver.1 = (f32[512,1024]{1,0:T(8,128)}, f32[512,1024]{1,0:T(8,128)}, f32[32,1024]{1,0:T(8,128)}, f32[32,1024]{1,0:T(8,128)}, f32[32,1024]{1,0:T(8,128)}, /*in...) custom-call(f32[512,1024]{1,0:T(8,128)} %get-tuple-element.71.refs_0_, ...), custom_call_target="tpu_custom_call" | custom-call | tf_op jit(solution)/shard_map/deliver/pallas_call | solution.py:1252
  389.7 0.7 slice.9
  (44 shorter events, 2.2 us)
Async XLA Ops:
  148.1 4.0 %slice-start = ((s8[5767168]{0:T(1024)(128)(4,1)}), s8[4194304]{0:T(1024)(128)(4,1)S(1)}, s32[]{:S(2)}) async-start(s8[5767168]{0:T(1024)(128)(4,1)} %bitcast.99), calls=%async_computation | async-start | bytes 8388608
  148.1 3.7 copy-start.3
  148.2 4.0 %slice-start.1 = ((s8[5767168]{0:T(1024)(128)(4,1)}), s8[1572864]{0:T(1024)(128)(4,1)S(1)}, s32[]{:S(2)}) async-start(s8[5767168]{0:T(1024)(128)(4,1)} %bitcast.99), calls=%async_computation.1 | async-start | bytes 3145728
  151.9 5.2 %slice-start.2 = ((s8[5767168]{0:T(1024)(128)(4,1)}), s8[4194304]{0:T(1024)(128)(4,1)S(1)}, s32[]{:S(2)}) async-start(s8[5767168]{0:T(1024)(128)(4,1)} %bitcast.103), calls=%async_computation.2 | async-start | bytes 8388608
  152.1 5.0 %slice-start.3 = ((s8[5767168]{0:T(1024)(128)(4,1)}), s8[1572864]{0:T(1024)(128)(4,1)S(1)}, s32[]{:S(2)}) async-start(s8[5767168]{0:T(1024)(128)(4,1)} %bitcast.103), calls=%async_computation.3 | async-start | bytes 3145728
  152.2 10.0 %slice-start.4 = ((s8[5767168]{0:T(1024)(128)(4,1)}), s8[4194304]{0:T(1024)(128)(4,1)S(1)}, s32[]{:S(2)}) async-start(s8[5767168]{0:T(1024)(128)(4,1)} %bitcast.107), calls=%async_computation.4 | async-start | bytes 8388608
  157.1 5.0 %copy-start.1 = (bf16[2,256,1024]{2,1,0:T(8,128)(2,1)S(1)}, bf16[2,256,1024]{2,1,0:T(8,128)(2,1)}, u32[]{:S(2)}) copy-start(bf16[2,256,1024]{2,1,0:T(8,128)(2,1)} %param.15) | copy-start | bytes 3145732
  157.1 5.0 %slice-start.5 = ((s8[5767168]{0:T(1024)(128)(4,1)}), s8[1572864]{0:T(1024)(128)(4,1)S(1)}, s32[]{:S(2)}) async-start(s8[5767168]{0:T(1024)(128)(4,1)} %bitcast.107), calls=%async_computation.5 | async-start | bytes 3145728
  172.1 6.1 %copy-start.6 = (bf16[512,2816]{1,0:T(8,128)(2,1)S(1)}, bf16[512,2816]{1,0:T(8,128)(2,1)}, u32[]{:S(2)}) copy-start(bf16[512,2816]{1,0:T(8,128)(2,1)} %get-tuple-element.95) | copy-start | bytes 8650756
  185.4 1.6 copy-start.4
  187.0 2.3 copy-start
  187.0 2.3 copy-start.2
  192.0 5.1 %copy-start.7 = (bf16[512,2816]{1,0:T(8,128)(2,1)S(1)}, bf16[512,2816]{1,0:T(8,128)(2,1)}, u32[]{:S(2)}) copy-start(bf16[512,2816]{1,0:T(8,128)(2,1)} %get-tuple-element.95) | copy-start | bytes 8650756
  197.0 5.1 %copy-start.5 = (bf16[512,2816]{1,0:T(8,128)(2,1)S(1)}, bf16[512,2816]{1,0:T(8,128)(2,1)}, u32[]{:S(2)}) copy-start(bf16[512,2816]{1,0:T(8,128)(2,1)} %get-tuple-element.96) | copy-start | bytes 8650756
